TPU v7x, 32 devices: a whole 2x2x4 slice. The times are simulated.
32 devices in a mesh: graph: 2 (over x), col: 4 (over z), row: 4 (over y, core).
Axes of the slice: x: 2, y: 2, z: 4, core: 2. Of those that a mesh axis runs over, the one named last changes fastest.
Arguments:
- flow_init: float32 [8192, 4096], P(('graph', 'row'), 'col'), parts along dimension 0
- flow_graph: float32 [8192, 4096], P(('graph', 'row'), 'col'), parts along dimension 0
Outputs:
- output: float32 [8192, 4096], P(('graph', 'row'), 'col'), parts along dimension 0
There are 2 independent parts. A program takes and returns all parts, laid end to end along the dimension named above; each array names one.
All inputs are finite; a program needn't handle non-finite values.
Results may differ from a plain program's by a relative error of at most 0.001.
Values are sent between devices in bfloat16 or wider.
A program may use at most 1 GiB of HBM per device.

v0:
```python
import jax
import jax.numpy as jnp
from jax import lax
from jax.sharding import PartitionSpec as P

ITERATIONS = 3


def solution(mesh):
    num_cols = mesh.shape["col"]
    block_spec = P(("graph", "row"), "col")

    def device_step(init_blk, graph_blk):
        mat_order = init_blk.shape[1] * num_cols
        graph_panel = lax.all_gather(graph_blk.astype(jnp.bfloat16), "row", axis=0, tiled=True)
        flow_blk = init_blk
        for _ in range(ITERATIONS):
            row_panel = lax.all_gather(flow_blk.astype(jnp.bfloat16), "col", axis=1, tiled=True)
            expanded = jnp.dot(row_panel, graph_panel, preferred_element_type=jnp.float32)
            inflated = expanded * expanded
            col_sum = lax.psum(jnp.sum(inflated, axis=0), "row")
            flow_blk = inflated * (mat_order / col_sum)
        return flow_blk

    return jax.shard_map(device_step, mesh=mesh, in_specs=(block_spec, block_spec), out_specs=block_spec, check_vma=False)
```

profile of v0, /device:TPU:0, one launch (start us, length us, event | category | flops | bytes accessed | tf_op | source)
XLA Modules:
  0.0 603.7 jit_solution(7913889643691522019)
XLA Ops:
  6.5 0.0 all-gather.5.cloned.1.call-start
  6.5 3.8 convert_element_type.12
  10.4 0.0 all-gather.5.cloned.1.call-update
  10.4 0.0 all-gather.7.cloned.1.call-start
  10.4 3.9 convert_element_type.13
  14.3 0.0 all-gather.7.cloned.1.call-update
  14.3 0.0 all-gather.9.cloned.1.call-start
  14.4 148.4 %all-gather.5.cloned.1.call-done = bf16[1024,4096]{1,0:T(8,128)(2,1)} async-done(((bf16[1024,1024]{1,0:T(8,128)(2,1)}), bf16[1024,4096]{1,0:T(8,128)(2,1)}) %all-gather.5.cloned.1.call-update) | async-done | bytes 8388624 | tf_op jit(solution)/shard_map/all_gather | solution.py:18
  162.8 58.5 %all-gather.7.cloned.1.call-done = bf16[4096,1024]{1,0:T(8,128)(2,1)} async-done(((bf16[1024,1024]{1,0:T(8,128)(2,1)}), bf16[4096,1024]{1,0:T(8,128)(2,1)}) %all-gather.7.cloned.1.call-update) | async-done | bytes 8388624 | tf_op jit(solution)/shard_map/all_gather | solution.py:15
  221.3 15.0 %multiply_reduce_fusion.2 = (f32[1024]{0:T(1024)S(1)}, f32[1024,1024]{1,0:T(8,128)}) fusion(bf16[1024,4096]{1,0:T(8,128)(2,1)} %all-gather.5.cloned.1.call-done, bf16[4096,1024]{1,0:T(8,128)(2,1)} %all-gather.7.cloned.1.call-done), kind=kOutput, calls=%fused_computation.5 | convolution fusion | flops 8592030720 | bytes 20975616 | tf_op jit(solution)/shard_map/dot_general | solution.py:19
  236.3 5.9 psum.21
  242.2 4.2 multiply_convert_fusion.1
  246.3 0.0 all-gather.9.cloned.1.call-update
  246.4 0.0 all-gather.11.cloned.1.call-start
  246.4 150.7 %all-gather.9.cloned.1.call-done = bf16[1024,4096]{1,0:T(8,128)(2,1)} async-done(((bf16[1024,1024]{1,0:T(8,128)(2,1)}), bf16[1024,4096]{1,0:T(8,128)(2,1)}) %all-gather.9.cloned.1.call-update) | async-done | bytes 8388624 | tf_op jit(solution)/shard_map/all_gather | solution.py:18
  397.1 15.0 %multiply_reduce_fusion.1 = (f32[1024]{0:T(1024)S(1)}, f32[1024,1024]{1,0:T(8,128)}) fusion(bf16[1024,4096]{1,0:T(8,128)(2,1)} %all-gather.9.cloned.1.call-done, bf16[4096,1024]{1,0:T(8,128)(2,1)} %all-gather.7.cloned.1.call-done), kind=kOutput, calls=%fused_computation.4 | convolution fusion | flops 8592030720 | bytes 20975616 | tf_op jit(solution)/shard_map/dot_general | solution.py:19
  412.0 6.8 %psum.22 = f32[1024]{0:T(1024)S(1)} all-reduce(f32[1024]{0:T(1024)S(1)} %get-tuple-element.7), channel_id=1, replica_groups=mesh['graph'=2,'col'=4,'row'=4] {'row'}, use_global_device_ids=true, to_apply=%region_3.0 | all-reduce | flops 1024 | bytes 8192 | tf_op jit(solution)/shard_map/psum | solution.py:21
  418.9 4.2 multiply_convert_fusion
  423.0 0.0 all-gather.11.cloned.1.call-update
  423.0 147.2 %all-gather.11.cloned.1.call-done = bf16[1024,4096]{1,0:T(8,128)(2,1)} async-done(((bf16[1024,1024]{1,0:T(8,128)(2,1)}), bf16[1024,4096]{1,0:T(8,128)(2,1)}) %all-gather.11.cloned.1.call-update) | async-done | bytes 8388624 | tf_op jit(solution)/shard_map/all_gather | solution.py:18
  570.2 15.0 %multiply_reduce_fusion = (f32[1024]{0:T(1024)S(1)}, f32[1024,1024]{1,0:T(8,128)}) fusion(bf16[1024,4096]{1,0:T(8,128)(2,1)} %all-gather.11.cloned.1.call-done, bf16[4096,1024]{1,0:T(8,128)(2,1)} %all-gather.7.cloned.1.call-done), kind=kOutput, calls=%fused_computation.3 | convolution fusion | flops 8592030720 | bytes 20975616 | tf_op jit(solution)/shard_map/dot_general | solution.py:19
  585.2 6.8 %psum.23 = f32[1024]{0:T(1024)S(1)} all-reduce(f32[1024]{0:T(1024)S(1)} %get-tuple-element.9), channel_id=1, replica_groups=mesh['graph'=2,'col'=4,'row'=4] {'row'}, use_global_device_ids=true, to_apply=%region_5.0 | all-reduce | flops 1024 | bytes 8192 | tf_op jit(solution)/shard_map/psum | solution.py:21
  592.0 5.1 multiply_multiply_fusion
  (3 shorter events, 0.0 us)
Async XLA Ops:
  6.5 156.3 %all-gather.5.cloned.1.call-start = ((), (), s32[]{:S(2)}) async-start(), calls=%async_computation | async-start | bytes 10485760 | tf_op jit(solution)/shard_map/all_gather | solution.py:18
  10.4 210.9 %all-gather.7.cloned.1.call-start = ((), (), s32[]{:S(2)}) async-start(), calls=%async_computation.1 | async-start | bytes 10485760 | tf_op jit(solution)/shard_map/all_gather | solution.py:15
  14.3 382.7 %all-gather.9.cloned.1.call-start = ((), (), s32[]{:S(2)}) async-start(), calls=%async_computation.2 | async-start | bytes 10485760 | tf_op jit(solution)/shard_map/all_gather | solution.py:18
  246.4 323.9 %all-gather.11.cloned.1.call-start = ((), (), s32[]{:S(2)}) async-start(), calls=%async_computation.3 | async-start | bytes 10485760 | tf_op jit(solution)/shard_map/all_gather | solution.py:18
Sparse Core Ops, SparseCore 0:
  10.5 152.2 all-gather.4
  164.4 56.9 all-gather.6
  246.5 150.5 all-gather.8
  423.2 146.9 all-gather.10
where the time goes:
time: 604 us
  waiting for transfers between devices  505 us (84%)
  matrix products  44.9 us (7%)
  other arithmetic  21.2 us (4%)
  blocking collectives  19.5 us (3%)
  between operations  13.1 us (2%)
    all_gather x3, waiting for transfers between devices, device_step(): lax.all_gather(flow_blk.astype(jnp.bfloat16), 'col', axis=1, tiled=True)  446 us
    all_gather x1, waiting for transfers between devices, device_step(): lax.all_gather(graph_blk.astype(jnp.bfloat16), 'row', axis=0, tiled=True)  58.5 us
    dot_general x3, matrix products, device_step(): jnp.dot(row_panel, graph_panel, preferred_element_type=jnp.float32)  44.9 us
    psum x3, blocking collectives, device_step(): col_sum = lax.psum(jnp.sum(inflated, axis=0), 'row')  19.5 us
    convert_element_type x3, other arithmetic, device_step(): flow_blk.astype(jnp.bfloat16)  12.1 us
  transfers between devices with their start and end apart: 4, of which 4 were waited for; matrix products, arithmetic and copies ran while one was open for 1% of the time, Pallas kernels for 0%

commit v1 on v0

v1 whole, which is shorter than its diff:
```python
import functools

import jax
import jax.numpy as jnp
from jax import lax
from jax.experimental import pallas as pl
from jax.experimental.pallas import tpu as pltpu
from jax.sharding import PartitionSpec as P

ITERATIONS = 3
CHUNKS = 8
TAIL_CHUNKS = 8
MESH = pl.DeviceIdType.MESH


def mcl_kernel(a_hbm, g_hbm, m_out, s_out, g, a, snd, acc, fin, psum, ar, sc, scin,
               load_sem, rg, rp, ra, send_sem, fin_send, ar_send, ar_recv, fin_recv, sc_sem, out_sem):
    n_col = g.shape[0]
    blk = g.shape[2]
    n = g.shape[1]
    half = blk // 2
    rows_c = blk // CHUNKS
    rows_t = half // TAIL_CHUNKS

    z = lax.axis_index("col")
    r = lax.axis_index("row")
    y = r // 2
    c = r % 2
    side = z // 2
    middle = jnp.logical_or(z == 1, z == 2)
    zm = 1 + side
    zc = 3 * side
    zmo = 2 - side
    zco = 3 - 3 * side
    r_y = 2 * (1 - y) + c
    r_p = 2 * y + 1 - c

    def dev(zq, rq):
        return {"col": zq, "row": rq}

    def remote(src, dst, ssem, rsem, d):
        return pltpu.make_async_remote_copy(
            src_ref=src, dst_ref=dst, send_sem=ssem, recv_sem=rsem, device_id=d, device_id_type=MESH)

    def g_piece(zq, rq, ch):
        return g.at[zq, pl.ds(pl.multiple_of(rq * blk + ch * rows_c, rows_c), rows_c), :]

    def g_block(zq, rq):
        return g.at[zq, pl.ds(pl.multiple_of(rq * blk, blk), blk), :]

    def send_g(link, zq, rq, ch, d):
        piece = g_piece(zq, rq, ch)
        remote(piece, piece, send_sem.at[link, zq, rq // 2], rg.at[zq, rq // 2, ch], d).start()

    def send_g_partner(zq, rq, ch):
        piece = g_piece(zq, rq, ch)
        remote(piece, piece, send_sem.at[2, zq, rq // 2], rp.at[zq, rq // 2, ch], dev(zm, r_p)).start()

    def wait_g(zq, rq, ch):
        piece = g_piece(zq, rq, ch)
        remote(piece, piece, send_sem.at[0, 0, 0], rg.at[zq, rq // 2, ch], dev(z, r)).wait_recv()

    def wait_g_partner(zq, rq, ch):
        piece = g_piece(zq, rq, ch)
        remote(piece, piece, send_sem.at[0, 0, 0], rp.at[zq, rq // 2, ch], dev(z, r)).wait_recv()

    def wait_sent(link, zq, rq):
        block = g_block(zq, rq)
        remote(block, block, send_sem.at[link, zq, rq // 2], rg.at[0, 0, 0], dev(z, r)).wait_send()

    def a_cols(zq):
        return a.at[:, pl.ds(pl.multiple_of(zq * blk, blk), blk)]

    def send_a(src, dst, link, idx, d):
        return remote(src, dst, send_sem.at[link, idx, 2], ra.at[idx], d)

    barrier = pltpu.get_barrier_semaphore()

    @pl.when(middle)
    def _():
        for dz in range(2):
            for dr in range(n_col):
                peer_z = zm if dz == 0 else zmo
                peer_r = (r + dr) % n_col
                if dz == 0 and dr == 0:
                    peer_z = zc
                pl.semaphore_signal(barrier, inc=1, device_id=dev(peer_z, peer_r), device_id_type=MESH)

    @pl.when(jnp.logical_not(middle))
    def _():
        pl.semaphore_signal(barrier, inc=1, device_id=dev(zm, r), device_id_type=MESH)
        pl.semaphore_signal(barrier, inc=1, device_id=dev(zc, r_y), device_id_type=MESH)

    loads = []
    for h in range(2):
        loads.append(pltpu.make_async_copy(g_hbm.at[pl.ds(h * half, half), :], acc.at[2 + h], load_sem.at[2 + h]))
    for h in range(2):
        loads.append(pltpu.make_async_copy(a_hbm.at[pl.ds(h * half, half), :], acc.at[h], load_sem.at[h]))
    for load in loads:
        load.start()
    for h in range(2):
        loads[h].wait()
        g[z, pl.ds(pl.multiple_of(r * blk + h * half, half), half), :] = acc[2 + h].astype(jnp.bfloat16)
    for h in range(2):
        loads[2 + h].wait()
    snd[0] = acc[1 - side].astype(jnp.bfloat16)
    a[:, pl.ds(pl.multiple_of(z * blk, blk), blk)] = acc[side].astype(jnp.bfloat16)

    @pl.when(jnp.logical_not(middle))
    def _():
        pl.semaphore_wait(barrier, 2)

        @pl.loop(0, CHUNKS)
        def _(ch):
            send_g(3, z, r, ch, dev(zm, r))
            send_g(1, z, r, ch, dev(zc, r_y))

        to_other = send_a(snd.at[0], snd.at[1], 3, 0, dev(zm, r))
        to_middle = send_a(a_cols(z), a_cols(z), 3, 1, dev(zm, r))
        to_other.start()
        to_middle.start()

        @pl.loop(0, CHUNKS)
        def _(ch):
            wait_g(z, r_y, ch)
            send_g(3, z, r_y, ch, dev(zm, r))

        wait_sent(3, z, r)
        wait_sent(1, z, r)
        wait_sent(3, z, r_y)
        to_other.wait_send()
        to_middle.wait_send()

        remote(fin.at[side], fin.at[side], fin_send.at[0], fin_recv.at[1, 0], dev(z, r)).wait_recv()
        own = pltpu.make_async_copy(fin.at[side], m_out.at[pl.ds(pl.multiple_of(side * half, half), half), :], out_sem.at[0])
        own.start()

        @pl.loop(0, TAIL_CHUNKS)
        def _(ch):
            piece = fin.at[1 - side, pl.ds(pl.multiple_of(ch * rows_t, rows_t), rows_t), :]
            remote(piece, piece, fin_send.at[0], fin_recv.at[2, ch], dev(z, r)).wait_recv()
            dst = m_out.at[pl.ds(pl.multiple_of((1 - side) * half + ch * rows_t, rows_t), rows_t), :]
            pltpu.make_async_copy(piece, dst, out_sem.at[1]).start()

        remote(scin, scin, sc_sem.at[0], sc_sem.at[1], dev(z, r)).wait_recv()
        scale_copy = pltpu.make_async_copy(scin, s_out, out_sem.at[2])
        scale_copy.start()
        own.wait()
        pltpu.make_async_copy(
            fin.at[1 - side], m_out.at[pl.ds(pl.multiple_of((1 - side) * half, half), half), :], out_sem.at[1]).wait()
        scale_copy.wait()

    @pl.when(middle)
    def _():
        pl.semaphore_wait(barrier, 2 * n_col)
        other = dev(zmo, r)
        across = dev(zm, r_y)
        corner = dev(zc, r)
        me = side * n_col + r

        @pl.loop(0, CHUNKS)
        def _(ch):
            send_g(0, zm, r, ch, other)
            send_g(1, zm, r, ch, across)
            send_g_partner(zm, r, ch)

        own_a = send_a(snd.at[0], a_cols(zm), 0, 2, other)
        own_a.start()

        @pl.loop(0, CHUNKS)
        def _(ch):
            wait_g(zmo, r, ch)
            send_g(1, zmo, r, ch, across)
            send_g_partner(zmo, r, ch)
            wait_g(zc, r, ch)
            send_g(0, zc, r, ch, other)
            send_g_partner(zc, r, ch)
            wait_g(zm, r_y, ch)
            send_g_partner(zm, r_y, ch)

        relay_a = send_a(snd.at[1], a_cols(zc), 0, 3, other)

        @pl.loop(0, CHUNKS // 2)
        def _(ch):
            wait_g(zmo, r_y, ch)
            send_g_partner(zmo, r_y, ch)

        remote(snd.at[1], snd.at[1], send_sem.at[0, 0, 2], ra.at[0], dev(z, r)).wait_recv()
        relay_a.start()

        @pl.loop(0, CHUNKS // 2)
        def _(ch):
            wait_g(zco, r, ch)
            send_g(1, zco, r, ch, across)
            send_g_partner(zco, r, ch)
            wait_g(zmo, r_y, ch + CHUNKS // 2)
            send_g_partner(zmo, r_y, ch + CHUNKS // 2)

        @pl.loop(0, CHUNKS)
        def _(ch):
            @pl.when(ch < CHUNKS // 2)
            def _():
                wait_g(zco, r, ch + CHUNKS // 2)
                send_g(1, zco, r, ch + CHUNKS // 2, across)
                send_g_partner(zco, r, ch + CHUNKS // 2)
            wait_g(zc, r_y, ch)
            send_g_partner(zc, r_y, ch)
            wait_g(zco, r_y, ch)
            send_g_partner(zco, r_y, ch)

        for idx, zq in ((1, zc), (2, zmo), (3, zco)):
            remote(a_cols(zq), a_cols(zq), send_sem.at[0, 0, 2], ra.at[idx], dev(z, r)).wait_recv()

        @pl.loop(0, CHUNKS)
        def _(ch):
            for zq in range(n_col):
                for yq in range(2):
                    wait_g_partner(zq, 2 * yq + 1 - c, ch)

        tile = 256
        per_block = blk // tile

        def expand(zq):
            @pl.loop(0, per_block)
            def _(j):
                cols = pl.ds(pl.multiple_of(j * tile, tile), tile)
                acc[zq, :, cols] = jnp.dot(a[...], g[zq, :, cols], preferred_element_type=jnp.float32)

        def inflate(t, zq):
            total = jnp.zeros((8, blk), jnp.float32)
            step = 64

            def body(i, total):
                rows = pl.ds(pl.multiple_of(i * step, step), step)
                value = acc[zq, rows, :]
                value = value * value
                acc[zq, rows, :] = value
                return total + jnp.sum(value.reshape(step // 8, 8, blk), axis=0)

            total = lax.fori_loop(0, half // step, body, total)
            psum[t, zq] = jnp.sum(total, axis=0, keepdims=True)

        def ar_copy(t, k, peer_z, peer_r):
            return remote(psum.at[t], ar.at[t, me], ar_send.at[t, k], ar_recv.at[t, me], dev(peer_z, peer_r))

        def peers():
            for dz in range(2):
                for dr in range(n_col):
                    if dz or dr:
                        yield dz * n_col + dr, (zmo if dz else zm), (r + dr) % n_col

        def column_scales(t):
            for k, pz, pr in peers():
                ar_copy(t, k, pz, pr).start()
            ar[t, me] = psum[t]
            for k, pz, pr in peers():
                src = (1 - side if k >= n_col else side) * n_col + pr
                remote(psum.at[t], ar.at[t, src], ar_send.at[t, k], ar_recv.at[t, src], dev(z, r)).wait_recv()
            total = ar[t, 0]
            for src in range(1, 2 * n_col):
                total = total + ar[t, src]
            sc[...] = n / total

        for t in range(ITERATIONS - 1):
            @pl.loop(0, n_col)
            def _(zq):
                expand(zq)
                inflate(t, zq)

            column_scales(t)

            @pl.loop(0, n_col)
            def _(zq):
                a[:, pl.ds(pl.multiple_of(zq * blk, blk), blk)] = (acc[zq] * sc[zq]).astype(jnp.bfloat16)

        t = ITERATIONS - 1
        expand(zco)
        inflate(t, zco)

        def tail_piece(ref, lead, ch):
            return ref.at[lead, pl.ds(pl.multiple_of(ch * rows_t, rows_t), rows_t), :]

        @pl.loop(0, TAIL_CHUNKS)
        def _(ch):
            remote(tail_piece(acc, zco, ch), tail_piece(fin, 1, ch), fin_send.at[0], fin_recv.at[2, ch], other).start()

        expand(zc)
        inflate(t, zc)
        to_corner = remote(acc.at[zc], fin.at[side], fin_send.at[1], fin_recv.at[1, 0], corner)
        to_corner.start()
        expand(zmo)
        inflate(t, zmo)
        to_other = remote(acc.at[zmo], fin.at[0], fin_send.at[2], fin_recv.at[0, 0], other)
        to_other.start()
        expand(zm)
        inflate(t, zm)
        own = pltpu.make_async_copy(acc.at[zm], m_out.at[pl.ds(pl.multiple_of(side * half, half), half), :], out_sem.at[0])
        own.start()
        column_scales(t)
        scale_corner = remote(sc.at[zc], scin, sc_sem.at[0], sc_sem.at[1], corner)
        scale_corner.start()
        scale_own = pltpu.make_async_copy(sc.at[zm], s_out, out_sem.at[2])
        scale_own.start()

        @pl.loop(0, TAIL_CHUNKS)
        def _(ch):
            piece = tail_piece(fin, 1, ch)
            remote(piece, piece, fin_send.at[0], fin_recv.at[2, ch], dev(z, r)).wait_recv()
            remote(piece, tail_piece(fin, 1 - side, ch), fin_send.at[3], fin_recv.at[2, ch], corner).start()

        remote(fin.at[0], fin.at[0], fin_send.at[0], fin_recv.at[0, 0], dev(z, r)).wait_recv()
        rest = pltpu.make_async_copy(
            fin.at[0], m_out.at[pl.ds(pl.multiple_of((1 - side) * half, half), half), :], out_sem.at[1])
        rest.start()

        wait_sent(0, zm, r)
        wait_sent(0, zc, r)
        wait_sent(1, zm, r)
        wait_sent(1, zmo, r)
        wait_sent(1, zco, r)
        for zq in range(n_col):
            for yq in range(2):
                wait_sent(2, zq, 2 * yq + c)
        own_a.wait_send()
        relay_a.wait_send()
        for t in range(ITERATIONS):
            for k, pz, pr in peers():
                ar_copy(t, k, pz, pr).wait_send()
        remote(acc.at[zco], fin.at[1], fin_send.at[0], fin_recv.at[0, 0], other).wait_send()
        to_corner.wait_send()
        to_other.wait_send()
        remote(fin.at[1], fin.at[1], fin_send.at[3], fin_recv.at[0, 0], corner).wait_send()
        scale_corner.wait_send()
        own.wait()
        rest.wait()
        scale_own.wait()


def solution(mesh):
    num_cols = mesh.shape["col"]
    num_rows = mesh.shape["row"]
    block_spec = P(("graph", "row"), "col")

    def device_step(init_blk, graph_blk):
        blk = init_blk.shape[0]
        n = blk * num_rows
        half = blk // 2
        any_spec = pl.BlockSpec(memory_space=pl.ANY)
        squares, scale = pl.pallas_call(
            mcl_kernel,
            out_shape=(jax.ShapeDtypeStruct((blk, blk), jnp.float32), jax.ShapeDtypeStruct((1, blk), jnp.float32)),
            in_specs=[any_spec, any_spec],
            out_specs=(any_spec, any_spec),
            scratch_shapes=[
                pltpu.VMEM((num_cols, n, blk), jnp.bfloat16),
                pltpu.VMEM((half, n), jnp.bfloat16),
                pltpu.VMEM((2, half, blk), jnp.bfloat16),
                pltpu.VMEM((num_cols, half, blk), jnp.float32),
                pltpu.VMEM((2, half, blk), jnp.float32),
                pltpu.VMEM((ITERATIONS, num_cols, 1, blk), jnp.float32),
                pltpu.VMEM((ITERATIONS, 2 * num_rows, num_cols, 1, blk), jnp.float32),
                pltpu.VMEM((num_cols, 1, blk), jnp.float32),
                pltpu.VMEM((1, blk), jnp.float32),
                pltpu.SemaphoreType.DMA((4,)),
                pltpu.SemaphoreType.DMA((num_cols, 2, CHUNKS)),
                pltpu.SemaphoreType.DMA((num_cols, 2, CHUNKS)),
                pltpu.SemaphoreType.DMA((4,)),
                pltpu.SemaphoreType.DMA((4, num_cols, 3)),
                pltpu.SemaphoreType.DMA((4,)),
                pltpu.SemaphoreType.DMA((ITERATIONS, 2 * num_rows)),
                pltpu.SemaphoreType.DMA((ITERATIONS, 2 * num_rows)),
                pltpu.SemaphoreType.DMA((3, TAIL_CHUNKS)),
                pltpu.SemaphoreType.DMA((2,)),
                pltpu.SemaphoreType.DMA((3,)),
            ],
            compiler_params=pltpu.CompilerParams(
                collective_id=0, has_side_effects=True, vmem_limit_bytes=67_000_000),
        )(init_blk, graph_blk)
        return squares * scale

    return jax.shard_map(device_step, mesh=mesh, in_specs=(block_spec, block_spec), out_specs=block_spec, check_vma=False)
```

time: 604 us -> 350 us (0.58)
  waiting for transfers between devices: 505 us -> 0 us
  Pallas kernels: 0 us -> 345 us
  matrix products: 44.9 us -> 0 us
  blocking collectives: 19.5 us -> 0 us
  other arithmetic: 21.2 us -> 4.78 us
  between operations: 13.1 us -> 0.01 us
    all_gather x4 -> x0, waiting for transfers between devices: 505 us -> none  [the longest x3 446 us: device_step(): lax.all_gather(flow_blk.astype(jnp.bfloat16), 'col', axis=1, tiled=True)]
    pallas_call x0 -> x1, Pallas kernels: none -> 345 us  [device_step(): pl.pallas_call(mcl_kernel, out_shape=(jax.ShapeDtypeStruct((blk, blk), jn...]
    dot_general x3 -> x0, matrix products: 44.9 us -> none  [device_step(): jnp.dot(row_panel, graph_panel, preferred_element_type=jnp.float32)]
    psum x3 -> x0, blocking collectives: 19.5 us -> none  [device_step(): col_sum = lax.psum(jnp.sum(inflated, axis=0), 'row')]
    convert_element_type x4 -> x0, other arithmetic: 16 us -> none  [the longest x3 12.1 us: device_step(): flow_blk.astype(jnp.bfloat16)]
  transfers between devices with their start and end apart: 4 -> 0, of which waited for: 4 -> 0; matrix products, arithmetic and copies ran while one was open for 1% -> 0% of each run, Pallas kernels for 0% -> 0%
where the time goes in v1:
time: 350 us
  Pallas kernels  345 us (99%)
  other arithmetic  4.78 us (1%)
    pallas_call x1, Pallas kernels, device_step(): pl.pallas_call(mcl_kernel, out_shape=(jax.ShapeDtypeStruct((blk, blk), jn...  345 us

profile of v1, /device:TPU:0, one launch (start us, length us, event | category | flops | bytes accessed | tf_op | source)
XLA Modules:
  0.0 350.0 jit_solution(17581279903434273347)
XLA Ops:
  0.0 345.2 %shard_map.28 = (f32[1024,1024]{1,0:T(8,128)}, f32[1,1024]{1,0:T(1,128)}) custom-call(f32[1024,1024]{1,0:T(8,128)} %a_hbm.1, f32[1024,1024]{1,0:T(8,128)} %g_hbm.1), custom_call_target="tpu_custom_call" | custom-call | tf_op jit(solution)/shard_map/pallas_call | solution.py:349
  345.2 4.8 %broadcast_multiply_fusion = f32[1024,1024]{1,0:T(8,128)} fusion(f32[1024,1024]{1,0:T(8,128)} %get-tuple-element.7, f32[1024]{0:T(1024)} %bitcast.1), kind=kLoop, calls=%fused_computation | loop fusion | flops 1048576 | bytes 8392704 | tf_op jit(solution)/shard_map/mul | solution.py:379

commit v2 on v1

--- a/solution.py
+++ b/solution.py
@@ -249,10 +249,12 @@
                     if dz or dr:
                         yield dz * n_col + dr, (zmo if dz else zm), (r + dr) % n_col
 
-        def column_scales(t):
+        def send_sums(t):
             for k, pz, pr in peers():
                 ar_copy(t, k, pz, pr).start()
             ar[t, me] = psum[t]
+
+        def column_scales(t):
             for k, pz, pr in peers():
                 src = (1 - side if k >= n_col else side) * n_col + pr
                 remote(psum.at[t], ar.at[t, src], ar_send.at[t, k], ar_recv.at[t, src], dev(z, r)).wait_recv()
@@ -267,6 +269,7 @@
                 expand(zq)
                 inflate(t, zq)
 
+            send_sums(t)
             column_scales(t)
 
             @pl.loop(0, n_col)
@@ -290,23 +293,25 @@
         to_corner.start()
         expand(zmo)
         inflate(t, zmo)
+        expand(zm)
+        inflate(t, zm)
+        send_sums(t)
         to_other = remote(acc.at[zmo], fin.at[0], fin_send.at[2], fin_recv.at[0, 0], other)
         to_other.start()
-        expand(zm)
-        inflate(t, zm)
         own = pltpu.make_async_copy(acc.at[zm], m_out.at[pl.ds(pl.multiple_of(side * half, half), half), :], out_sem.at[0])
         own.start()
+
+        @pl.loop(0, TAIL_CHUNKS)
+        def _(ch):
+            piece = tail_piece(fin, 1, ch)
+            remote(piece, piece, fin_send.at[0], fin_recv.at[2, ch], dev(z, r)).wait_recv()
+            remote(piece, tail_piece(fin, 1 - side, ch), fin_send.at[3], fin_recv.at[2, ch], corner).start()
+
         column_scales(t)
         scale_corner = remote(sc.at[zc], scin, sc_sem.at[0], sc_sem.at[1], corner)
         scale_corner.start()
         scale_own = pltpu.make_async_copy(sc.at[zm], s_out, out_sem.at[2])
         scale_own.start()
-
-        @pl.loop(0, TAIL_CHUNKS)
-        def _(ch):
-            piece = tail_piece(fin, 1, ch)
-            remote(piece, piece, fin_send.at[0], fin_recv.at[2, ch], dev(z, r)).wait_recv()
-            remote(piece, tail_piece(fin, 1 - side, ch), fin_send.at[3], fin_recv.at[2, ch], corner).start()
 
         remote(fin.at[0], fin.at[0], fin_send.at[0], fin_recv.at[0, 0], dev(z, r)).wait_recv()
         rest = pltpu.make_async_copy(

time: 350 us -> 306 us (0.87)
  Pallas kernels: 345 us -> 301 us
    pallas_call x1, Pallas kernels: 345 us -> 301 us  [device_step(): pl.pallas_call(mcl_kernel, out_shape=(jax.ShapeDtypeStruct((blk, blk), jn...]
where the time goes in v2:
time: 306 us
  Pallas kernels  301 us (98%)
  other arithmetic  4.78 us (2%)
    pallas_call x1, Pallas kernels, device_step(): pl.pallas_call(mcl_kernel, out_shape=(jax.ShapeDtypeStruct((blk, blk), jn...  301 us

profile of v2, /device:TPU:0, one launch (start us, length us, event | category | flops | bytes accessed | tf_op | source)
XLA Modules:
  0.0 306.1 jit_solution(4760719154576043333)
XLA Ops:
  0.0 301.3 %shard_map.28 = (f32[1024,1024]{1,0:T(8,128)}, f32[1,1024]{1,0:T(1,128)}) custom-call(f32[1024,1024]{1,0:T(8,128)} %a_hbm.1, f32[1024,1024]{1,0:T(8,128)} %g_hbm.1), custom_call_target="tpu_custom_call" | custom-call | tf_op jit(solution)/shard_map/pallas_call | solution.py:354
  301.3 4.8 %broadcast_multiply_fusion = f32[1024,1024]{1,0:T(8,128)} fusion(f32[1024,1024]{1,0:T(8,128)} %get-tuple-element.7, f32[1024]{0:T(1024)} %bitcast.1), kind=kLoop, calls=%fused_computation | loop fusion | flops 1048576 | bytes 8392704 | tf_op jit(solution)/shard_map/mul | solution.py:384

commit v3 on v0

v3 whole, which is shorter than its diff:
```python
import jax
import jax.numpy as jnp
from jax import lax
from jax.experimental import pallas as pl
from jax.experimental.pallas import tpu as pltpu
from jax.sharding import PartitionSpec as P

SUBS = 4
TILE = 256
AHEAD = 2
MESH = pl.DeviceIdType.MESH


def mcl_kernel(a_hbm, g_hbm, m_out, s_out, g, a, a1, snd, acc, fin, ps_mid, ar_mid, ps_edge, ar_edge, ps, ar, sc, scin,
               load_sem, rg, rp, ra, send_sem, fin_send, ar_send, ar_recv, fin_recv, sc_sem, out_sem):
    n_col = g.shape[0]
    blk = g.shape[2]
    n = g.shape[1]
    half = blk // 2
    pieces = blk // TILE
    rows_s = blk // SUBS
    rows_a = half // SUBS

    z = lax.axis_index("col")
    r = lax.axis_index("row")
    y = r // 2
    c = r % 2
    side = z // 2
    middle = jnp.logical_or(z == 1, z == 2)
    zm = 1 + side
    zc = 3 * side
    zmo = 2 - side
    zco = 3 - 3 * side
    r_y = 2 * (1 - y) + c
    r_p = 2 * y + 1 - c

    def dev(zq, rq):
        return {"col": zq, "row": rq}

    def remote(src, dst, ssem, rsem, d):
        return pltpu.make_async_remote_copy(
            src_ref=src, dst_ref=dst, send_sem=ssem, recv_sem=rsem, device_id=d, device_id_type=MESH)

    def cols(j):
        return pl.ds(pl.multiple_of(j * TILE, TILE), TILE)

    def g_sub(zq, rq, j, s):
        return g.at[zq, pl.ds(pl.multiple_of(rq * blk + s * rows_s, rows_s), rows_s), cols(j)]

    def g_piece(zq, rq, j):
        return g.at[zq, pl.ds(pl.multiple_of(rq * blk, blk), blk), cols(j)]

    def g_block(zq, rq):
        return g.at[zq, pl.ds(pl.multiple_of(rq * blk, blk), blk), :]

    def send_sub(link, zq, rq, j, s, d):
        ref = g_sub(zq, rq, j, s)
        remote(ref, ref, send_sem.at[link, zq, rq // 2], rg.at[zq, rq // 2, j, s], d).start()

    def wait_sub(zq, rq, j, s):
        ref = g_sub(zq, rq, j, s)
        remote(ref, ref, send_sem.at[0, 0, 0], rg.at[zq, rq // 2, j, s], dev(z, r)).wait_recv()

    def send_partner(zq, rq, j):
        ref = g_piece(zq, rq, j)
        remote(ref, ref, send_sem.at[2, zq, rq // 2], rp.at[zq, rq // 2, j], dev(zm, r_p)).start()

    def wait_partner(zq, j):
        for yq in range(2):
            ref = g_piece(zq, 2 * yq + 1 - c, j)
            remote(ref, ref, send_sem.at[0, 0, 0], rp.at[zq, yq, j], dev(z, r)).wait_recv()

    def wait_sent(link, zq, rq):
        block = g_block(zq, rq)
        remote(block, block, send_sem.at[link, zq, rq // 2], rg.at[0, 0, 0, 0], dev(z, r)).wait_send()

    def quarter(zq):
        return pl.ds(pl.multiple_of(zq * blk, blk), blk)

    def a_sub(s):
        return pl.ds(pl.multiple_of(s * rows_a, rows_a), rows_a)

    def send_a(idx, src, dst, link, s, d):
        remote(src.at[a_sub(s), :], dst.at[a_sub(s), :], send_sem.at[link, idx, 2], ra.at[idx, s], d).start()

    def wait_a(idx, s):
        ref = snd.at[1, a_sub(s), :]
        remote(ref, ref, send_sem.at[0, 0, 2], ra.at[idx, s], dev(z, r)).wait_recv()

    def wait_a_sent(idx, link):
        remote(snd.at[1], snd.at[1], send_sem.at[link, idx, 2], ra.at[0, 0], dev(z, r)).wait_send()

    barrier = pltpu.get_barrier_semaphore()

    @pl.when(middle)
    def _():
        for dz in range(2):
            for dr in range(n_col):
                peer_z = zm if dz == 0 else zmo
                if dz == 0 and dr == 0:
                    peer_z = zc
                pl.semaphore_signal(barrier, inc=1, device_id=dev(peer_z, (r + dr) % n_col), device_id_type=MESH)

    @pl.when(jnp.logical_not(middle))
    def _():
        pl.semaphore_signal(barrier, inc=1, device_id=dev(zm, r), device_id_type=MESH)
        pl.semaphore_signal(barrier, inc=1, device_id=dev(zc, r_y), device_id_type=MESH)

    loads = []
    for h in range(2):
        loads.append(pltpu.make_async_copy(a_hbm.at[pl.ds(h * half, half), :], acc.at[h], load_sem.at[h]))
    for h in range(2):
        loads.append(pltpu.make_async_copy(g_hbm.at[pl.ds(h * half, half), :], acc.at[2 + h], load_sem.at[2 + h]))
    for load in loads:
        load.start()
    for h in range(2):
        loads[h].wait()
    snd[0] = acc[1 - side].astype(jnp.bfloat16)
    a[:, quarter(z)] = acc[side].astype(jnp.bfloat16)
    for h in range(2):
        loads[2 + h].wait()
        g[z, pl.ds(pl.multiple_of(r * blk + h * half, half), half), :] = acc[2 + h].astype(jnp.bfloat16)

    def a_quarter(zq):
        return a.at[:, quarter(zq)]

    def out_rows(h):
        return pl.ds(pl.multiple_of(h * half, half), half)

    @pl.when(jnp.logical_not(middle))
    def _():
        pl.semaphore_wait(barrier, 2)
        inner = dev(zm, r)

        @pl.loop(0, SUBS)
        def _(s):
            send_a(0, snd.at[0], snd.at[1], 3, s, inner)

        @pl.loop(0, SUBS)
        def _(s):
            send_a(1, a_quarter(z), a_quarter(z), 3, s, inner)

        @pl.loop(0, pieces * SUBS)
        def _(i):
            send_sub(1, z, r, i // SUBS, i % SUBS, dev(zc, r_y))
            send_sub(3, z, r, i // SUBS, i % SUBS, inner)

        @pl.loop(0, pieces * SUBS)
        def _(i):
            wait_sub(z, r_y, i // SUBS, i % SUBS)
            send_sub(3, z, r_y, i // SUBS, i % SUBS, inner)

        wait_a_sent(0, 3)
        wait_a_sent(1, 3)
        wait_sent(3, z, r)
        wait_sent(1, z, r)
        wait_sent(3, z, r_y)

        for kind, h in ((1, side), (2, 1 - side)):
            @pl.loop(0, pieces)
            def _(j):
                ref = fin.at[h, :, cols(j)]
                remote(ref, ref, fin_send.at[0], fin_recv.at[kind, j], dev(z, r)).wait_recv()
                pltpu.make_async_copy(ref, m_out.at[out_rows(h), cols(j)], out_sem.at[kind - 1]).start()

        remote(scin, scin, sc_sem.at[0], sc_sem.at[1], dev(z, r)).wait_recv()
        scale_copy = pltpu.make_async_copy(scin, s_out, out_sem.at[2])
        scale_copy.start()
        for kind, h in ((1, side), (2, 1 - side)):
            pltpu.make_async_copy(fin.at[h], m_out.at[out_rows(h), :], out_sem.at[kind - 1]).wait()
        scale_copy.wait()

    @pl.when(middle)
    def _():
        pl.semaphore_wait(barrier, 2 * n_col)
        other = dev(zmo, r)
        across = dev(zm, r_y)
        corner = dev(zc, r)
        me = side * n_col + r

        def peers():
            for dz in range(2):
                for dr in range(n_col):
                    if dz or dr:
                        yield dz * n_col + dr, (zmo if dz else zm), (r + dr) % n_col

        def sums_of(i):
            if i == 0:
                return ps_mid, ar_mid
            if i <= pieces:
                return ps_edge.at[i - 1], ar_edge.at[i - 1]
            return ps.at[i - pieces - 1], ar.at[i - pieces - 1]

        def send_sums(i):
            src, slots = sums_of(i)
            for k, pz, pr in peers():
                remote(src, slots.at[me], ar_send.at[i, k], ar_recv.at[i, me], dev(pz, pr)).start()
            slots[me] = src[...]

        def scales(i):
            src, slots = sums_of(i)
            for k, pz, pr in peers():
                peer = (1 - side if k >= n_col else side) * n_col + pr
                remote(src, slots.at[peer], ar_send.at[i, k], ar_recv.at[i, peer], dev(z, r)).wait_recv()
            total = slots[0]
            for peer in range(1, 2 * n_col):
                total = total + slots[peer]
            return n / total

        def square(zq, j, slot):
            step = 64

            def body(i, total):
                rows = pl.ds(pl.multiple_of(i * step, step), step)
                value = acc[zq, rows, cols(j)]
                value = value * value
                acc[zq, rows, cols(j)] = value
                return total + jnp.sum(value.reshape(step // 8, 8, TILE), axis=0)

            total = lax.fori_loop(0, half // step, body, jnp.zeros((8, TILE), jnp.float32))
            slot[...] = jnp.sum(total, axis=0, keepdims=True)

        def expand(zq, j, slot):
            acc[zq, :, cols(j)] = jnp.dot(a[...], g[zq, :, cols(j)], preferred_element_type=jnp.float32)
            square(zq, j, slot)

        @pl.loop(0, SUBS)
        def _(s):
            send_a(2, snd.at[0], a_quarter(zm), 0, s, other)

        @pl.loop(0, pieces)
        def _(j):
            send_partner(zm, r, j)
            for s in range(SUBS):
                send_sub(1, zm, r, j, s, across)

        @pl.loop(0, SUBS)
        def _(s):
            wait_a(0, s)
            send_a(3, snd.at[1], a_quarter(zc), 0, s, other)

        @pl.loop(0, pieces * SUBS)
        def _(i):
            send_sub(0, zm, r, i // SUBS, i % SUBS, other)

        @pl.loop(0, pieces)
        def _(j):
            for s in range(SUBS):
                wait_sub(zm, r_y, j, s)
            send_partner(zm, r_y, j)

        @pl.loop(0, SUBS)
        def _(s):
            for idx in (2, 3, 1):
                wait_a(idx, s)

        @pl.loop(0, pieces)
        def _(j):
            @pl.loop(0, SUBS)
            def _(s):
                wait_sub(zmo, r, j, s)
                send_sub(1, zmo, r, j, s, across)
                wait_sub(zc, r, j, s)
                wait_sub(zmo, r_y, j, s)

                @pl.when(s == SUBS - 1)
                def _():
                    send_partner(zmo, r, j)
                    send_partner(zc, r, j)
                    send_partner(zmo, r_y, j)

                late = s // 2
                zq = zm + late * (zmo - zm)
                jq = j - late

                @pl.when(jnp.logical_and(s % 2 == 0, jq >= 0))
                def _():
                    wait_partner(zq, jq)
                    expand(zq, jq, ps_mid.at[zq - 1, :, cols(jq)])

        def finish_mid():
            scale = scales(0)
            for idx, zq in ((0, 1), (1, 2)):
                a1[:, pl.ds(zq * blk, blk)] = (acc[zq] * scale[idx]).astype(jnp.bfloat16)

        def finish_edge(j):
            scale = scales(1 + j)
            for idx, zq in ((0, 0), (1, 3)):
                a1[:, pl.ds(zq * blk + j * TILE, TILE)] = (
                    acc[zq, :, pl.ds(j * TILE, TILE)] * scale[idx]).astype(jnp.bfloat16)

        def partial(zq, k0, k_len, n0, n_len):
            rows = pl.ds(pl.multiple_of(k0, TILE), k_len)
            return jnp.dot(a1[:, rows], g[zq, rows, pl.ds(pl.multiple_of(n0, TILE), n_len)],
                           preferred_element_type=jnp.float32)

        def mid_by_mid(zq):
            @pl.loop(0, pieces)
            def _(j):
                acc[zq, :, cols(j)] = (partial(zq, blk, blk, j * TILE, TILE) + partial(zq, 2 * blk, blk, j * TILE, TILE))

        def new_columns(j):
            @pl.loop(0, 2)
            def _(i):
                zq = 3 * i
                total = partial(zq, blk, blk, j * TILE, TILE) + partial(zq, 2 * blk, blk, j * TILE, TILE)
                for k_z in (0, 3):
                    total += partial(zq, k_z * blk, (j + 1) * TILE, j * TILE, TILE)
                acc[zq, :, pl.ds(j * TILE, TILE)] = total

        def old_columns(j):
            def add(zq, n0, n_len):
                span = pl.ds(pl.multiple_of(n0, TILE), n_len)
                acc[zq, :, span] += (partial(zq, j * TILE, TILE, n0, n_len)
                                     + partial(zq, 3 * blk + j * TILE, TILE, n0, n_len))

            wide = 2 * TILE

            @pl.loop(0, 2 * blk // wide)
            def _(i):
                per = blk // wide
                add(1 + i // per, (i % per) * wide, wide)

            if j:
                @pl.loop(0, 2 * j)
                def _(i):
                    add(3 * (i // j), (i % j) * TILE, TILE)

        for i in range(AHEAD):
            send_sub(0, zc, r, i // SUBS, i % SUBS, other)

        for j in range(pieces):
            def pump(s):
                ahead = j * SUBS + s + AHEAD

                @pl.when(ahead < pieces * SUBS)
                def _():
                    send_sub(0, zc, r, ahead // SUBS, ahead % SUBS, other)

                wait_sub(zco, r, j, s)
                send_sub(1, zco, r, j, s, across)
                wait_sub(zc, r_y, j, s)
                wait_sub(zco, r_y, j, s)

            @pl.loop(0, 2)
            def _(s):
                pump(s)
                if j:
                    zq = zc + s * (zco - zc)
                    wait_partner(zq, j - 1)
                    expand(zq, j - 1, ps_edge.at[j - 1, zq // 3])
                else:
                    @pl.when(s == 0)
                    def _():
                        wait_partner(zmo, pieces - 1)
                        expand(zmo, pieces - 1, ps_mid.at[zmo - 1, :, cols(pieces - 1)])

            send_sums(j)
            pump(2)
            if j == 1:
                finish_mid()
                mid_by_mid(1)
            elif j > 1:
                finish_edge(j - 2)
                new_columns(j - 2)
            pump(3)
            send_partner(zco, r, j)
            send_partner(zc, r_y, j)
            send_partner(zco, r_y, j)
            if j == 1:
                mid_by_mid(2)
            elif j > 1:
                old_columns(j - 2)

        last = pieces - 1

        @pl.loop(0, 2)
        def _(s):
            zq = zc + s * (zco - zc)
            wait_partner(zq, last)
            expand(zq, last, ps_edge.at[last, zq // 3])

        send_sums(pieces)
        for j in (last - 1, last):
            finish_edge(j)
            new_columns(j)
            old_columns(j)

        @pl.loop(0, n_col)
        def _(zq):
            for j in range(pieces):
                square(zq, j, ps.at[0, zq, :, cols(j)])

        send_sums(pieces + 1)
        sc[...] = scales(pieces + 1)

        @pl.loop(0, n_col)
        def _(zq):
            a[:, quarter(zq)] = (acc[zq] * sc[zq]).astype(jnp.bfloat16)

        def fin_piece(ref, lead, j):
            return ref.at[lead, :, cols(j)]

        @pl.loop(0, pieces)
        def _(j):
            @pl.loop(0, 2)
            def _(i):
                zq = zco + i * (zc - zco)
                expand(zq, j, ps.at[1, zq, :, cols(j)])

                @pl.when(i == 0)
                def _():
                    remote(fin_piece(acc, zco, j), fin_piece(fin, 1, j), fin_send.at[0], fin_recv.at[2, j], other).start()

                @pl.when(i == 1)
                def _():
                    remote(fin_piece(acc, zc, j), fin_piece(fin, side, j), fin_send.at[1], fin_recv.at[1, j], corner).start()

        @pl.loop(0, 2 * pieces)
        def _(i):
            zq = zmo + (i // pieces) * (zm - zmo)
            j = i % pieces
            expand(zq, j, ps.at[1, zq, :, cols(j)])

        send_sums(pieces + 2)
        to_other = remote(acc.at[zmo], fin.at[0], fin_send.at[2], fin_recv.at[0, 0], other)
        to_other.start()
        own = pltpu.make_async_copy(acc.at[zm], m_out.at[out_rows(side), :], out_sem.at[0])
        own.start()

        @pl.loop(0, pieces)
        def _(j):
            ref = fin_piece(fin, 1, j)
            remote(ref, ref, fin_send.at[0], fin_recv.at[2, j], dev(z, r)).wait_recv()
            remote(ref, fin_piece(fin, 1 - side, j), fin_send.at[3], fin_recv.at[2, j], corner).start()

        sc[...] = scales(pieces + 2)
        scale_corner = remote(sc.at[zc], scin, sc_sem.at[0], sc_sem.at[1], corner)
        scale_corner.start()
        scale_own = pltpu.make_async_copy(sc.at[zm], s_out, out_sem.at[2])
        scale_own.start()

        remote(fin.at[0], fin.at[0], fin_send.at[0], fin_recv.at[0, 0], dev(z, r)).wait_recv()
        rest = pltpu.make_async_copy(fin.at[0], m_out.at[out_rows(1 - side), :], out_sem.at[1])
        rest.start()

        wait_a_sent(2, 0)
        wait_a_sent(3, 0)
        wait_sent(0, zm, r)
        wait_sent(0, zc, r)
        wait_sent(1, zm, r)
        wait_sent(1, zmo, r)
        wait_sent(1, zco, r)
        for zq in range(n_col):
            for yq in range(2):
                wait_sent(2, zq, 2 * yq + c)
        for i in range(pieces + 3):
            src, slots = sums_of(i)
            for k, pz, pr in peers():
                remote(src, slots.at[me], ar_send.at[i, k], ar_recv.at[i, me], dev(pz, pr)).wait_send()
        remote(acc.at[zco], fin.at[1], fin_send.at[0], fin_recv.at[0, 0], other).wait_send()
        remote(acc.at[zc], fin.at[side], fin_send.at[1], fin_recv.at[0, 0], corner).wait_send()
        to_other.wait_send()
        remote(fin.at[1], fin.at[1], fin_send.at[3], fin_recv.at[0, 0], corner).wait_send()
        scale_corner.wait_send()
        own.wait()
        rest.wait()
        scale_own.wait()


def solution(mesh):
    num_cols = mesh.shape["col"]
    num_rows = mesh.shape["row"]
    block_spec = P(("graph", "row"), "col")

    def device_step(init_blk, graph_blk):
        blk = init_blk.shape[0]
        n = blk * num_rows
        half = blk // 2
        pieces = blk // TILE
        cores = 2 * num_rows
        any_spec = pl.BlockSpec(memory_space=pl.ANY)
        squares, scale = pl.pallas_call(
            mcl_kernel,
            out_shape=(jax.ShapeDtypeStruct((blk, blk), jnp.float32), jax.ShapeDtypeStruct((1, blk), jnp.float32)),
            in_specs=[any_spec, any_spec],
            out_specs=(any_spec, any_spec),
            scratch_shapes=[
                pltpu.VMEM((num_cols, n, blk), jnp.bfloat16),
                pltpu.VMEM((half, n), jnp.bfloat16),
                pltpu.VMEM((half, n), jnp.bfloat16),
                pltpu.VMEM((2, half, blk), jnp.bfloat16),
                pltpu.VMEM((num_cols, half, blk), jnp.float32),
                pltpu.VMEM((2, half, blk), jnp.float32),
                pltpu.VMEM((2, 1, blk), jnp.float32),
                pltpu.VMEM((cores, 2, 1, blk), jnp.float32),
                pltpu.VMEM((pieces, 2, 1, TILE), jnp.float32),
                pltpu.VMEM((pieces, cores, 2, 1, TILE), jnp.float32),
                pltpu.VMEM((2, num_cols, 1, blk), jnp.float32),
                pltpu.VMEM((2, cores, num_cols, 1, blk), jnp.float32),
                pltpu.VMEM((num_cols, 1, blk), jnp.float32),
                pltpu.VMEM((1, blk), jnp.float32),
                pltpu.SemaphoreType.DMA((4,)),
                pltpu.SemaphoreType.DMA((num_cols, 2, pieces, SUBS)),
                pltpu.SemaphoreType.DMA((num_cols, 2, pieces)),
                pltpu.SemaphoreType.DMA((4, SUBS)),
                pltpu.SemaphoreType.DMA((4, num_cols, 3)),
                pltpu.SemaphoreType.DMA((4,)),
                pltpu.SemaphoreType.DMA((pieces + 3, cores)),
                pltpu.SemaphoreType.DMA((pieces + 3, cores)),
                pltpu.SemaphoreType.DMA((3, pieces)),
                pltpu.SemaphoreType.DMA((2,)),
                pltpu.SemaphoreType.DMA((3,)),
            ],
            compiler_params=pltpu.CompilerParams(
                collective_id=0, has_side_effects=True, vmem_limit_bytes=67_000_000),
        )(init_blk, graph_blk)
        return squares * scale

    return jax.shard_map(device_step, mesh=mesh, in_specs=(block_spec, block_spec), out_specs=block_spec, check_vma=False)
```

time: 604 us -> 362 us (0.60)
  waiting for transfers between devices: 505 us -> 0 us
  Pallas kernels: 0 us -> 357 us
  matrix products: 44.9 us -> 0 us
  blocking collectives: 19.5 us -> 0 us
  other arithmetic: 21.2 us -> 4.78 us
  between operations: 13.1 us -> 0.01 us
    all_gather x4 -> x0, waiting for transfers between devices: 505 us -> none  [the longest x3 446 us: device_step(): lax.all_gather(flow_blk.astype(jnp.bfloat16), 'col', axis=1, tiled=True)]
    pallas_call x0 -> x1, Pallas kernels: none -> 357 us  [device_step(): pl.pallas_call(mcl_kernel, out_shape=(jax.ShapeDtypeStruct((blk, blk), jn...]
    dot_general x3 -> x0, matrix products: 44.9 us -> none  [device_step(): jnp.dot(row_panel, graph_panel, preferred_element_type=jnp.float32)]
    psum x3 -> x0, blocking collectives: 19.5 us -> none  [device_step(): col_sum = lax.psum(jnp.sum(inflated, axis=0), 'row')]
    convert_element_type x4 -> x0, other arithmetic: 16 us -> none  [the longest x3 12.1 us: device_step(): flow_blk.astype(jnp.bfloat16)]
  transfers between devices with their start and end apart: 4 -> 0, of which waited for: 4 -> 0; matrix products, arithmetic and copies ran while one was open for 1% -> 0% of each run, Pallas kernels for 0% -> 0%
where the time goes in v3:
time: 362 us
  Pallas kernels  357 us (99%)
  other arithmetic  4.78 us (1%)
    pallas_call x1, Pallas kernels, device_step(): pl.pallas_call(mcl_kernel, out_shape=(jax.ShapeDtypeStruct((blk, blk), jn...  357 us

profile of v3, /device:TPU:0, one launch (start us, length us, event | category | flops | bytes accessed | tf_op | source)
XLA Modules:
  0.0 361.8 jit_solution(4943662713611231071)
XLA Ops:
  0.0 357.1 %shard_map.28 = (f32[1024,1024]{1,0:T(8,128)}, f32[1,1024]{1,0:T(1,128)}) custom-call(f32[1024,1024]{1,0:T(8,128)} %a_hbm.1, f32[1024,1024]{1,0:T(8,128)} %g_hbm.1), custom_call_target="tpu_custom_call" | custom-call | tf_op jit(solution)/shard_map/pallas_call | solution.py:483
  357.1 4.8 %broadcast_multiply_fusion = f32[1024,1024]{1,0:T(8,128)} fusion(f32[1024,1024]{1,0:T(8,128)} %get-tuple-element.7, f32[1024]{0:T(1024)} %bitcast.1), kind=kLoop, calls=%fused_computation | loop fusion | flops 1048576 | bytes 8392704 | tf_op jit(solution)/shard_map/mul | solution.py:518

commit v4 on v3

--- a/solution.py
+++ b/solution.py
@@ -7,7 +7,8 @@
 
 SUBS = 4
 TILE = 256
-AHEAD = 2
+AHEAD = 3
+LAG = 3
 MESH = pl.DeviceIdType.MESH
 
 
@@ -254,30 +255,6 @@
             for idx in (2, 3, 1):
                 wait_a(idx, s)
 
-        @pl.loop(0, pieces)
-        def _(j):
-            @pl.loop(0, SUBS)
-            def _(s):
-                wait_sub(zmo, r, j, s)
-                send_sub(1, zmo, r, j, s, across)
-                wait_sub(zc, r, j, s)
-                wait_sub(zmo, r_y, j, s)
-
-                @pl.when(s == SUBS - 1)
-                def _():
-                    send_partner(zmo, r, j)
-                    send_partner(zc, r, j)
-                    send_partner(zmo, r_y, j)
-
-                late = s // 2
-                zq = zm + late * (zmo - zm)
-                jq = j - late
-
-                @pl.when(jnp.logical_and(s % 2 == 0, jq >= 0))
-                def _():
-                    wait_partner(zq, jq)
-                    expand(zq, jq, ps_mid.at[zq - 1, :, cols(jq)])
-
         def finish_mid():
             scale = scales(0)
             for idx, zq in ((0, 1), (1, 2)):
@@ -326,53 +303,98 @@
                 def _(i):
                     add(3 * (i // j), (i % j) * TILE, TILE)
 
-        for i in range(AHEAD):
-            send_sub(0, zc, r, i // SUBS, i % SUBS, other)
-
-        for j in range(pieces):
-            def pump(s):
-                ahead = j * SUBS + s + AHEAD
-
-                @pl.when(ahead < pieces * SUBS)
+        n_slices = pieces * SUBS
+
+        def from_other(q):
+            return zmo + (q // pieces) * (zco - zmo)
+
+        def pump(i):
+            q, s = i // SUBS, i % SUBS
+            j = q % pieces
+            z_m = from_other(q)
+            r_e = r + (q // pieces) * (r_y - r)
+            ahead = i + AHEAD - n_slices
+
+            @pl.when(jnp.logical_and(ahead >= 0, ahead < n_slices))
+            def _():
+                send_sub(0, zc, r, ahead // SUBS, ahead % SUBS, other)
+
+            wait_sub(z_m, r, j, s)
+            send_sub(1, z_m, r, j, s, across)
+            wait_sub(zc, r_e, j, s)
+
+            @pl.when(s == SUBS - 1)
+            def _():
+                send_partner(z_m, r, j)
+                send_partner(zc, r_e, j)
+
+            @pl.when(i >= LAG)
+            def _():
+                pump_across(i - LAG)
+
+        def pump_across(i):
+            q, s = i // SUBS, i % SUBS
+            wait_sub(from_other(q), r_y, q % pieces, s)
+
+            @pl.when(s == SUBS - 1)
+            def _():
+                send_partner(from_other(q), r_y, q % pieces)
+
+        @pl.loop(0, pieces + 1)
+        def _(q):
+            @pl.loop(0, SUBS)
+            def _(s):
+                pump(q * SUBS + s)
+                first = q == 0
+                zq = jnp.where(first, zm, zmo)
+                jq = jnp.where(first, s, q - 1)
+
+                @pl.when(jnp.logical_or(first, s == SUBS - 1))
                 def _():
-                    send_sub(0, zc, r, ahead // SUBS, ahead % SUBS, other)
-
-                wait_sub(zco, r, j, s)
-                send_sub(1, zco, r, j, s, across)
-                wait_sub(zc, r_y, j, s)
-                wait_sub(zco, r_y, j, s)
-
-            @pl.loop(0, 2)
+                    wait_partner(zq, jq)
+                    expand(zq, jq, ps_mid.at[zq - 1, :, cols(jq)])
+
+        send_sums(0)
+
+        def edge_step(j, second, third):
+            @pl.loop(0, SUBS)
             def _(s):
-                pump(s)
-                if j:
-                    zq = zc + s * (zco - zc)
-                    wait_partner(zq, j - 1)
-                    expand(zq, j - 1, ps_edge.at[j - 1, zq // 3])
-                else:
-                    @pl.when(s == 0)
-                    def _():
-                        wait_partner(zmo, pieces - 1)
-                        expand(zmo, pieces - 1, ps_mid.at[zmo - 1, :, cols(pieces - 1)])
-
-            send_sums(j)
-            pump(2)
-            if j == 1:
-                finish_mid()
-                mid_by_mid(1)
-            elif j > 1:
-                finish_edge(j - 2)
-                new_columns(j - 2)
-            pump(3)
-            send_partner(zco, r, j)
-            send_partner(zc, r_y, j)
-            send_partner(zco, r_y, j)
-            if j == 1:
-                mid_by_mid(2)
-            elif j > 1:
-                old_columns(j - 2)
+                pump((pieces + 1 + j) * SUBS + s)
+
+                @pl.when(jnp.logical_or(s == 0, s == SUBS - 1))
+                def _():
+                    zq = jnp.where(s == 0, zc, zco)
+                    wait_partner(zq, j)
+                    expand(zq, j, ps_edge.at[j, zq // 3])
+
+                @pl.when(s == 1)
+                def _():
+                    second()
+
+                @pl.when(s == 2)
+                def _():
+                    third()
+
+            send_sums(1 + j)
+
+        def mid_start():
+            finish_mid()
+            mid_by_mid(1)
+
+        def edge_start(j):
+            finish_edge(j)
+            new_columns(j)
+
+        edge_step(0, lambda: None, mid_start)
+        edge_step(1, lambda: mid_by_mid(2), lambda: None)
+        edge_step(2, lambda: edge_start(0), lambda: old_columns(0))
 
         last = pieces - 1
+        edge_start(last - 2)
+        old_columns(last - 2)
+        for i in range(2 * n_slices - LAG, 2 * n_slices):
+            pump_across(i)
+        edge_start(last - 1)
 
         @pl.loop(0, 2)
         def _(s):
@@ -381,10 +403,9 @@
             expand(zq, last, ps_edge.at[last, zq // 3])
 
         send_sums(pieces)
-        for j in (last - 1, last):
-            finish_edge(j)
-            new_columns(j)
-            old_columns(j)
+        old_columns(last - 1)
+        edge_start(last)
+        old_columns(last)
 
         @pl.loop(0, n_col)
         def _(zq):

time: 362 us -> 275 us (0.76)
  Pallas kernels: 357 us -> 270 us
    pallas_call x1, Pallas kernels: 357 us -> 270 us  [device_step(): pl.pallas_call(mcl_kernel, out_shape=(jax.ShapeDtypeStruct((blk, blk), jn...]
where the time goes in v4:
time: 275 us
  Pallas kernels  270 us (98%)
  other arithmetic  4.78 us (2%)
    pallas_call x1, Pallas kernels, device_step(): pl.pallas_call(mcl_kernel, out_shape=(jax.ShapeDtypeStruct((blk, blk), jn...  270 us

profile of v4, /device:TPU:0, one launch (start us, length us, event | category | flops | bytes accessed | tf_op | source)
XLA Modules:
  0.0 274.7 jit_solution(17490249371454279848)
XLA Ops:
  0.0 269.9 %shard_map.28 = (f32[1024,1024]{1,0:T(8,128)}, f32[1,1024]{1,0:T(1,128)}) custom-call(f32[1024,1024]{1,0:T(8,128)} %a_hbm.1, f32[1024,1024]{1,0:T(8,128)} %g_hbm.1), custom_call_target="tpu_custom_call" | custom-call | tf_op jit(solution)/shard_map/pallas_call | solution.py:504
  269.9 4.8 %broadcast_multiply_fusion = f32[1024,1024]{1,0:T(8,128)} fusion(f32[1024,1024]{1,0:T(8,128)} %get-tuple-element.7, f32[1024]{0:T(1024)} %bitcast.1), kind=kLoop, calls=%fused_computation | loop fusion | flops 1048576 | bytes 8392704 | tf_op jit(solution)/shard_map/mul | solution.py:539

commit v5 on v4

v5 whole, which is shorter than its diff:
```python
import jax
import jax.numpy as jnp
from jax import lax
from jax.experimental import pallas as pl
from jax.experimental.pallas import tpu as pltpu
from jax.sharding import PartitionSpec as P

SUBS = 4
TILE = 256
AHEAD = 2
LAG = 3
MESH = pl.DeviceIdType.MESH


def mcl_kernel(a_hbm, g_hbm, m_out, s_out, g, a, a1, snd, acc, fin, ps_mid, ar_mid, ps_edge, ar_edge, ps, ar, sc,
               load_sem, rm, re, ry, rp, ra_relay, ra, send_sem, fin_send, ar_send, ar_recv, fin_recv, sc_sem):
    n_col = g.shape[0]
    blk = g.shape[2]
    n = g.shape[1]
    half = blk // 2
    pieces = blk // TILE
    rows_s = blk // SUBS
    rows_a = half // SUBS

    z = lax.axis_index("col")
    r = lax.axis_index("row")
    y = r // 2
    c = r % 2
    side = z // 2
    middle = jnp.logical_or(z == 1, z == 2)
    zm = 1 + side
    zc = 3 * side
    zmo = 2 - side
    zco = 3 - 3 * side
    r_y = 2 * (1 - y) + c
    r_p = 2 * y + 1 - c

    def dev(zq, rq):
        return {"col": zq, "row": rq}

    def remote(src, dst, ssem, rsem, d):
        return pltpu.make_async_remote_copy(
            src_ref=src, dst_ref=dst, send_sem=ssem, recv_sem=rsem, device_id=d, device_id_type=MESH)

    def cols(j):
        return pl.ds(pl.multiple_of(j * TILE, TILE), TILE)

    def g_sub(zq, rq, j, s):
        return g.at[zq, pl.ds(pl.multiple_of(rq * blk + s * rows_s, rows_s), rows_s), cols(j)]

    def g_piece(zq, rq, j):
        return g.at[zq, pl.ds(pl.multiple_of(rq * blk, blk), blk), cols(j)]

    def g_block(zq, rq):
        return g.at[zq, pl.ds(pl.multiple_of(rq * blk, blk), blk), :]

    def copy_to(ref, ssem, rsem, d):
        remote(ref, ref, ssem, rsem, d).start()

    def wait_for(ref, rsem):
        remote(ref, ref, send_sem.at[0], rsem, dev(z, r)).wait_recv()

    def wait_sent(ref, ssem):
        remote(ref, ref, ssem, re.at[0, 0], dev(z, r)).wait_send()

    def send_partner(zq, rq, j):
        copy_to(g_piece(zq, rq, j), send_sem.at[4 + zq], rp.at[zq, j], dev(zm, r_p))

    def wait_partner(zq, j):
        wait_for(g.at[zq, pl.ds(0, 2 * blk), cols(j)], rp.at[zq, j])

    def quarter(zq):
        return pl.ds(pl.multiple_of(zq * blk, blk), blk)

    def a_quarter(zq):
        return a.at[:, quarter(zq)]

    def a_sub(s):
        return pl.ds(pl.multiple_of(s * rows_a, rows_a), rows_a)

    def out_rows(h):
        return pl.ds(pl.multiple_of(h * half, half), half)

    barrier = pltpu.get_barrier_semaphore()

    @pl.when(middle)
    def _():
        for dz in range(2):
            for dr in range(n_col):
                peer_z = zm if dz == 0 else zmo
                if dz == 0 and dr == 0:
                    peer_z = zc
                pl.semaphore_signal(barrier, inc=1, device_id=dev(peer_z, (r + dr) % n_col), device_id_type=MESH)

    @pl.when(jnp.logical_not(middle))
    def _():
        pl.semaphore_signal(barrier, inc=1, device_id=dev(zm, r), device_id_type=MESH)
        pl.semaphore_signal(barrier, inc=1, device_id=dev(zc, r_y), device_id_type=MESH)

    def load(src, h, slot):
        return pltpu.make_async_copy(src.at[out_rows(h), :], acc.at[slot], load_sem.at[slot])

    loads = (load(a_hbm, 1 - side, 0), load(g_hbm, 0, 1), load(g_hbm, 1, 2), load(a_hbm, side, 3))
    for copy in loads:
        copy.start()
    loads[0].wait()
    snd[0] = acc[0].astype(jnp.bfloat16)
    pl.semaphore_wait(barrier, jnp.where(middle, 2 * n_col, 2))

    @pl.when(middle)
    def _():
        remote(snd.at[0], a_quarter(zm), send_sem.at[3], ra.at[1], dev(zmo, r)).start()

    @pl.when(jnp.logical_not(middle))
    def _():
        @pl.loop(0, SUBS)
        def _(s):
            remote(snd.at[0, a_sub(s), :], snd.at[1, a_sub(s), :], send_sem.at[3], ra_relay.at[s], dev(zm, r)).start()

    for h in range(2):
        loads[1 + h].wait()
        g[z, pl.ds(pl.multiple_of(r * blk + h * half, half), half), :] = acc[1 + h].astype(jnp.bfloat16)

    @pl.when(jnp.logical_not(middle))
    def _():
        inner = dev(zm, r)

        @pl.loop(0, pieces)
        def _(j):
            copy_to(g_piece(z, r, j), send_sem.at[1], ry.at[0, j], dev(zc, r_y))

        loads[3].wait()
        a[:, quarter(z)] = acc[3].astype(jnp.bfloat16)
        remote(a_quarter(z), a_quarter(z), send_sem.at[3], ra.at[0], inner).start()

        @pl.loop(0, pieces)
        def _(j):
            copy_to(g_piece(z, r, j), send_sem.at[2], re.at[0, j], inner)

        @pl.loop(0, pieces)
        def _(j):
            wait_for(g_piece(z, r_y, j), ry.at[0, j])
            copy_to(g_piece(z, r_y, j), send_sem.at[2], re.at[1, j], inner)

        wait_sent(snd, send_sem.at[3])
        wait_sent(g_block(z, r), send_sem.at[1])
        wait_sent(g.at[0, pl.ds(0, 2 * blk), :], send_sem.at[2])

        for kind, h in ((1, side), (2, 1 - side)):
            @pl.loop(0, pieces)
            def _(j):
                wait_for(m_out.at[out_rows(h), cols(j)], fin_recv.at[kind, j])

        wait_for(s_out, sc_sem.at[1])

    @pl.when(middle)
    def _():
        other = dev(zmo, r)
        across = dev(zm, r_y)
        corner = dev(zc, r)
        me = side * n_col + r

        def peers():
            for dz in range(2):
                for dr in range(n_col):
                    if dz or dr:
                        yield (zmo if dz else zm), (r + dr) % n_col

        def sums_of(i):
            if i == 0:
                return ps_mid, ar_mid
            if i <= pieces:
                return ps_edge.at[i - 1], ar_edge.at[i - 1]
            return ps.at[i - pieces - 1], ar.at[i - pieces - 1]

        def send_sums(i):
            src, slots = sums_of(i)
            for pz, pr in peers():
                remote(src, slots.at[me], ar_send.at[i], ar_recv.at[i], dev(pz, pr)).start()
            slots[me] = src[...]

        def peer_slots(i):
            return sums_of(i)[1].at[pl.ds(0, 2 * n_col - 1)]

        def scales(i):
            src, slots = sums_of(i)
            wait_for(peer_slots(i), ar_recv.at[i])
            total = slots[0]
            for peer in range(1, 2 * n_col):
                total = total + slots[peer]
            return n / total

        def square(zq, j, slot):
            step = 64

            def body(i, total):
                rows = pl.ds(pl.multiple_of(i * step, step), step)
                value = acc[zq, rows, cols(j)]
                value = value * value
                acc[zq, rows, cols(j)] = value
                return total + jnp.sum(value.reshape(step // 8, 8, TILE), axis=0)

            total = lax.fori_loop(0, half // step, body, jnp.zeros((8, TILE), jnp.float32))
            slot[...] = jnp.sum(total, axis=0, keepdims=True)

        def expand(zq, j, slot):
            acc[zq, :, cols(j)] = jnp.dot(a[...], g[zq, :, cols(j)], preferred_element_type=jnp.float32)
            square(zq, j, slot)

        @pl.loop(0, pieces)
        def _(j):
            copy_to(g_piece(zm, r, j), send_sem.at[1], ry.at[0, j], across)
            send_partner(zm, r, j)

        loads[3].wait()
        a[:, quarter(zm)] = acc[3].astype(jnp.bfloat16)

        @pl.loop(0, SUBS)
        def _(s):
            wait_for(snd.at[1, a_sub(s), :], ra_relay.at[s])
            remote(snd.at[1, a_sub(s), :], a.at[a_sub(s), quarter(zc)], send_sem.at[3], ra.at[2], other).start()

        @pl.loop(0, pieces * SUBS)
        def _(i):
            copy_to(g_sub(zm, r, i // SUBS, i % SUBS), send_sem.at[0], rm.at[0, i // SUBS, i % SUBS], other)

        @pl.loop(0, pieces)
        def _(j):
            wait_for(g_piece(zm, r_y, j), ry.at[0, j])
            send_partner(zm, r_y, j)

        for idx, zq in ((1, zmo), (2, zco), (0, zc)):
            wait_for(a_quarter(zq), ra.at[idx])

        def finish_mid():
            scale = scales(0)
            for idx, zq in ((0, 1), (1, 2)):
                a1[:, pl.ds(zq * blk, blk)] = (acc[zq] * scale[idx]).astype(jnp.bfloat16)

        def finish_edge(j):
            scale = scales(1 + j)
            for idx, zq in ((0, 0), (1, 3)):
                a1[:, pl.ds(zq * blk + j * TILE, TILE)] = (
                    acc[zq, :, pl.ds(j * TILE, TILE)] * scale[idx]).astype(jnp.bfloat16)

        def partial(zq, k0, k_len, n0, n_len):
            rows = pl.ds(pl.multiple_of(k0, TILE), k_len)
            return jnp.dot(a1[:, rows], g[zq, rows, pl.ds(pl.multiple_of(n0, TILE), n_len)],
                           preferred_element_type=jnp.float32)

        def mid_by_mid(zq):
            @pl.loop(0, pieces)
            def _(j):
                acc[zq, :, cols(j)] = (partial(zq, blk, blk, j * TILE, TILE) + partial(zq, 2 * blk, blk, j * TILE, TILE))

        def new_columns(j):
            @pl.loop(0, 2)
            def _(i):
                zq = 3 * i
                total = partial(zq, blk, blk, j * TILE, TILE) + partial(zq, 2 * blk, blk, j * TILE, TILE)
                for k_z in (0, 3):
                    total += partial(zq, k_z * blk, (j + 1) * TILE, j * TILE, TILE)
                acc[zq, :, pl.ds(j * TILE, TILE)] = total

        def old_columns(j):
            def add(zq, n0, n_len):
                span = pl.ds(pl.multiple_of(n0, TILE), n_len)
                acc[zq, :, span] += (partial(zq, j * TILE, TILE, n0, n_len)
                                     + partial(zq, 3 * blk + j * TILE, TILE, n0, n_len))

            wide = 2 * TILE

            @pl.loop(0, 2 * blk // wide)
            def _(i):
                per = blk // wide
                add(1 + i // per, (i % per) * wide, wide)

            if j:
                @pl.loop(0, 2 * j)
                def _(i):
                    add(3 * (i // j), (i % j) * TILE, TILE)

        n_slices = pieces * SUBS

        def from_other(q):
            return zmo + (q // pieces) * (zco - zmo)

        def pump(i):
            q, s = i // SUBS, i % SUBS
            late, j = q // pieces, q % pieces
            z_m = from_other(q)
            ahead = i + AHEAD - n_slices

            @pl.when(jnp.logical_and(ahead >= 0, ahead < n_slices))
            def _():
                ref = g_sub(zc, r, ahead // SUBS, ahead % SUBS)
                copy_to(ref, send_sem.at[0], rm.at[1, ahead // SUBS, ahead % SUBS], other)

            ref = g_sub(z_m, r, j, s)
            wait_for(ref, rm.at[late, j, s])
            copy_to(ref, send_sem.at[1], ry.at[1 + late, j], across)

            @pl.when(s == SUBS - 1)
            def _():
                r_e = r + late * (r_y - r)
                send_partner(z_m, r, j)
                wait_for(g_piece(zc, r_e, j), re.at[late, j])
                send_partner(zc, r_e, j)

            @pl.when(jnp.logical_and(i >= LAG, (i - LAG) % SUBS == SUBS - 1))
            def _():
                piece_across((i - LAG) // SUBS)

        def piece_across(q):
            late, j = q // pieces, q % pieces
            wait_for(g_piece(from_other(q), r_y, j), ry.at[1 + late, j])
            send_partner(from_other(q), r_y, j)

        @pl.loop(0, pieces + 1)
        def _(q):
            @pl.loop(0, SUBS)
            def _(s):
                pump(q * SUBS + s)
                first = q == 0
                zq = jnp.where(first, zm, zmo)
                jq = jnp.where(first, s, q - 1)

                @pl.when(jnp.logical_or(first, s == SUBS - 1))
                def _():
                    wait_partner(zq, jq)
                    expand(zq, jq, ps_mid.at[zq - 1, :, cols(jq)])

        send_sums(0)

        def edge_step(j, second, third, fourth):
            @pl.loop(0, SUBS)
            def _(s):
                pump((pieces + 1 + j) * SUBS + s)

                @pl.when(jnp.logical_or(s == 0, s == SUBS - 1))
                def _():
                    zq = jnp.where(s == 0, zc, zco)
                    wait_partner(zq, j)
                    expand(zq, j, ps_edge.at[j, zq // 3])

                @pl.when(s == 1)
                def _():
                    second()

                @pl.when(s == 2)
                def _():
                    third()

            send_sums(1 + j)
            fourth()

        def mid_start():
            finish_mid()
            mid_by_mid(1)

        def edge_start(j):
            finish_edge(j)
            new_columns(j)

        def idle():
            pass

        edge_step(0, idle, mid_start, idle)
        edge_step(1, lambda: mid_by_mid(2), lambda: edge_start(0), idle)
        edge_step(2, lambda: old_columns(0), lambda: edge_start(1), lambda: old_columns(1))

        last = pieces - 1

        def last_piece(zq):
            wait_partner(zq, last)
            expand(zq, last, ps_edge.at[last, zq // 3])

        last_piece(zc)
        piece_across(2 * pieces - 1)
        edge_start(last - 1)
        last_piece(zco)
        send_sums(pieces)
        old_columns(last - 1)
        edge_start(last)
        old_columns(last)

        @pl.loop(0, n_col)
        def _(zq):
            for j in range(pieces):
                square(zq, j, ps.at[0, zq, :, cols(j)])

        send_sums(pieces + 1)
        sc[...] = scales(pieces + 1)

        @pl.loop(0, n_col)
        def _(zq):
            a[:, quarter(zq)] = (acc[zq] * sc[zq]).astype(jnp.bfloat16)

        @pl.loop(0, pieces)
        def _(j):
            @pl.loop(0, 2)
            def _(i):
                zq = zco + i * (zc - zco)
                expand(zq, j, ps.at[1, zq, :, cols(j)])
                done = acc.at[zq, :, cols(j)]

                @pl.when(i == 0)
                def _():
                    remote(done, fin.at[:, cols(j)], fin_send.at[0], fin_recv.at[2, j], other).start()

                @pl.when(i == 1)
                def _():
                    remote(done, m_out.at[out_rows(side), cols(j)], fin_send.at[1], fin_recv.at[1, j], corner).start()

        @pl.loop(0, 2 * pieces)
        def _(i):
            zq = zmo + (i // pieces) * (zm - zmo)
            j = i % pieces
            expand(zq, j, ps.at[1, zq, :, cols(j)])

        send_sums(pieces + 2)
        remote(acc.at[zmo], m_out.at[out_rows(side), :], fin_send.at[2], fin_recv.at[0, 0], other).start()
        m_out[out_rows(side), :] = acc[zm]

        @pl.loop(0, pieces)
        def _(j):
            ref = fin.at[:, cols(j)]
            wait_for(ref, fin_recv.at[2, j])
            remote(ref, m_out.at[out_rows(1 - side), cols(j)], fin_send.at[3], fin_recv.at[2, j], corner).start()

        sc[...] = scales(pieces + 2)
        remote(sc.at[zc], s_out, sc_sem.at[0], sc_sem.at[1], corner).start()
        s_out[...] = sc[zm]

        wait_sent(snd, send_sem.at[3])
        wait_sent(g.at[0, pl.ds(0, 2 * blk), :], send_sem.at[0])
        wait_sent(g.at[0, pl.ds(0, 3 * blk), :], send_sem.at[1])
        for zq in range(n_col):
            wait_sent(g.at[0, pl.ds(0, 2 * blk), :], send_sem.at[4 + zq])
        for i in range(pieces + 3):
            wait_sent(peer_slots(i), ar_send.at[i])
        for i in range(4):
            wait_sent(acc.at[0], fin_send.at[i])
        wait_sent(sc.at[0], sc_sem.at[0])
        wait_for(m_out.at[out_rows(1 - side), :], fin_recv.at[0, 0])


def solution(mesh):
    num_cols = mesh.shape["col"]
    num_rows = mesh.shape["row"]
    block_spec = P(("graph", "row"), "col")

    def device_step(init_blk, graph_blk):
        blk = init_blk.shape[0]
        n = blk * num_rows
        half = blk // 2
        pieces = blk // TILE
        cores = 2 * num_rows
        any_spec = pl.BlockSpec(memory_space=pl.ANY)
        vmem_spec = pl.BlockSpec(memory_space=pltpu.VMEM)
        squares, scale = pl.pallas_call(
            mcl_kernel,
            out_shape=(pltpu.VMEM((blk, blk), jnp.float32), pltpu.VMEM((1, blk), jnp.float32)),
            in_specs=[any_spec, any_spec],
            out_specs=(vmem_spec, vmem_spec),
            scratch_shapes=[
                pltpu.VMEM((num_cols, n, blk), jnp.bfloat16),
                pltpu.VMEM((half, n), jnp.bfloat16),
                pltpu.VMEM((half, n), jnp.bfloat16),
                pltpu.VMEM((2, half, blk), jnp.bfloat16),
                pltpu.VMEM((num_cols, half, blk), jnp.float32),
                pltpu.VMEM((half, blk), jnp.float32),
                pltpu.VMEM((2, 1, blk), jnp.float32),
                pltpu.VMEM((cores, 2, 1, blk), jnp.float32),
                pltpu.VMEM((pieces, 2, 1, TILE), jnp.float32),
                pltpu.VMEM((pieces, cores, 2, 1, TILE), jnp.float32),
                pltpu.VMEM((2, num_cols, 1, blk), jnp.float32),
                pltpu.VMEM((2, cores, num_cols, 1, blk), jnp.float32),
                pltpu.VMEM((num_cols, 1, blk), jnp.float32),
                pltpu.SemaphoreType.DMA((4,)),
                pltpu.SemaphoreType.DMA((2, pieces, SUBS)),
                pltpu.SemaphoreType.DMA((2, pieces)),
                pltpu.SemaphoreType.DMA((3, pieces)),
                pltpu.SemaphoreType.DMA((num_cols, pieces)),
                pltpu.SemaphoreType.DMA((SUBS,)),
                pltpu.SemaphoreType.DMA((3,)),
                pltpu.SemaphoreType.DMA((4 + num_cols,)),
                pltpu.SemaphoreType.DMA((4,)),
                pltpu.SemaphoreType.DMA((pieces + 3,)),
                pltpu.SemaphoreType.DMA((pieces + 3,)),
                pltpu.SemaphoreType.DMA((3, pieces)),
                pltpu.SemaphoreType.DMA((2,)),
            ],
            compiler_params=pltpu.CompilerParams(
                collective_id=0, has_side_effects=True, vmem_limit_bytes=60_000_000),
        )(init_blk, graph_blk)
        return squares * scale

    return jax.shard_map(device_step, mesh=mesh, in_specs=(block_spec, block_spec), out_specs=block_spec, check_vma=False)
```

time: 275 us -> 266 us (0.967)
  Pallas kernels: 270 us -> 263 us
    pallas_call x1, Pallas kernels: 270 us -> 263 us  [device_step(): pl.pallas_call(mcl_kernel, out_shape=(pltpu.VMEM((blk, blk), jnp.float32)...]
where the time goes in v5:
time: 266 us; the launch traced here: 265 us
  Pallas kernels  263 us (99%)
    pallas_call x1, Pallas kernels, device_step(): pl.pallas_call(mcl_kernel, out_shape=(pltpu.VMEM((blk, blk), jnp.float32)...  263 us

profile of v5, /device:TPU:0, one launch (start us, length us, event | category | flops | bytes accessed | tf_op | source)
XLA Modules:
  0.0 265.4 jit_solution(7562557505770303170)
XLA Ops:
  0.0 262.9 %shard_map.28 = (f32[1024,1024]{1,0:T(8,128)S(1)}, f32[1,1024]{1,0:T(1,128)S(1)}) custom-call(f32[1024,1024]{1,0:T(8,128)} %a_hbm.1, f32[1024,1024]{1,0:T(8,128)} %g_hbm.1), custom_call_target="tpu_custom_call" | custom-call | tf_op jit(solution)/shard_map/pallas_call | solution.py:461
  262.9 2.5 broadcast_multiply_fusion

commit v6 on v5

--- a/solution.py
+++ b/solution.py
@@ -166,12 +166,13 @@
                     if dz or dr:
                         yield (zmo if dz else zm), (r + dr) % n_col
 
+        exchanges = [(ps_mid.at[0], ar_mid.at[0])]
+        exchanges += [(ps_edge.at[j], ar_edge.at[j]) for j in range(pieces)]
+        exchanges += [(ps_mid.at[1], ar_mid.at[1]), (ps_mid.at[2], ar_mid.at[2]), (ps, ar)]
+        second_mid, second_edge, third = pieces + 1, pieces + 2, pieces + 3
+
         def sums_of(i):
-            if i == 0:
-                return ps_mid, ar_mid
-            if i <= pieces:
-                return ps_edge.at[i - 1], ar_edge.at[i - 1]
-            return ps.at[i - pieces - 1], ar.at[i - pieces - 1]
+            return exchanges[i]
 
         def send_sums(i):
             src, slots = sums_of(i)
@@ -190,22 +191,13 @@
                 total = total + slots[peer]
             return n / total
 
-        def square(zq, j, slot):
-            step = 64
-
-            def body(i, total):
-                rows = pl.ds(pl.multiple_of(i * step, step), step)
-                value = acc[zq, rows, cols(j)]
-                value = value * value
-                acc[zq, rows, cols(j)] = value
-                return total + jnp.sum(value.reshape(step // 8, 8, TILE), axis=0)
-
-            total = lax.fori_loop(0, half // step, body, jnp.zeros((8, TILE), jnp.float32))
-            slot[...] = jnp.sum(total, axis=0, keepdims=True)
+        def square(value, zq, span, slot):
+            value = value * value
+            acc[zq, :, span] = value
+            slot[...] = jnp.sum(value, axis=0, keepdims=True)
 
         def expand(zq, j, slot):
-            acc[zq, :, cols(j)] = jnp.dot(a[...], g[zq, :, cols(j)], preferred_element_type=jnp.float32)
-            square(zq, j, slot)
+            square(jnp.dot(a[...], g[zq, :, cols(j)], preferred_element_type=jnp.float32), zq, cols(j), slot)
 
         @pl.loop(0, pieces)
         def _(j):
@@ -243,42 +235,51 @@
                 a1[:, pl.ds(zq * blk + j * TILE, TILE)] = (
                     acc[zq, :, pl.ds(j * TILE, TILE)] * scale[idx]).astype(jnp.bfloat16)
 
-        def partial(zq, k0, k_len, n0, n_len):
-            rows = pl.ds(pl.multiple_of(k0, TILE), k_len)
-            return jnp.dot(a1[:, rows], g[zq, rows, pl.ds(pl.multiple_of(n0, TILE), n_len)],
+        def partial(rows, zq, k0, k_len, n0, n_len):
+            k = pl.ds(pl.multiple_of(k0, TILE), k_len)
+            return jnp.dot(rows[:, k], g[zq, k, pl.ds(pl.multiple_of(n0, TILE), n_len)],
                            preferred_element_type=jnp.float32)
+
+        def two_quarters(rows, zq, k_len, n0, *k_z):
+            first, second = (partial(rows, zq, k * blk, k_len, n0, TILE) for k in k_z)
+            return first + second
 
         def mid_by_mid(zq):
             @pl.loop(0, pieces)
             def _(j):
-                acc[zq, :, cols(j)] = (partial(zq, blk, blk, j * TILE, TILE) + partial(zq, 2 * blk, blk, j * TILE, TILE))
+                acc[zq, :, cols(j)] = two_quarters(a1, zq, blk, j * TILE, 1, 2)
 
         def new_columns(j):
             @pl.loop(0, 2)
             def _(i):
                 zq = 3 * i
-                total = partial(zq, blk, blk, j * TILE, TILE) + partial(zq, 2 * blk, blk, j * TILE, TILE)
-                for k_z in (0, 3):
-                    total += partial(zq, k_z * blk, (j + 1) * TILE, j * TILE, TILE)
-                acc[zq, :, pl.ds(j * TILE, TILE)] = total
-
-        def old_columns(j):
-            def add(zq, n0, n_len):
-                span = pl.ds(pl.multiple_of(n0, TILE), n_len)
-                acc[zq, :, span] += (partial(zq, j * TILE, TILE, n0, n_len)
-                                     + partial(zq, 3 * blk + j * TILE, TILE, n0, n_len))
-
-            wide = 2 * TILE
-
-            @pl.loop(0, 2 * blk // wide)
+                span = pl.ds(j * TILE, TILE)
+                total = (two_quarters(a1, zq, blk, j * TILE, 1, 2)
+                         + two_quarters(a1, zq, (j + 1) * TILE, j * TILE, 0, 3))
+                if j == pieces - 1:
+                    square(total, zq, span, ps_mid.at[2, i, :, span])
+                else:
+                    acc[zq, :, span] = total
+
+        def old_columns(j, zq, width, slot):
+            span = pl.ds(0, width)
+            total = (acc[zq, :, span] + partial(a1, zq, j * TILE, TILE, 0, width)
+                     + partial(a1, zq, 3 * blk + j * TILE, TILE, 0, width))
+            if j == pieces - 1:
+                square(total, zq, span, slot.at[:, span])
+            else:
+                acc[zq, :, span] = total
+
+        def old_mid(j):
+            @pl.loop(0, 2)
             def _(i):
-                per = blk // wide
-                add(1 + i // per, (i % per) * wide, wide)
-
+                old_columns(j, 1 + i, blk, ps_mid.at[1, i])
+
+        def old_edge(j):
             if j:
-                @pl.loop(0, 2 * j)
+                @pl.loop(0, 2)
                 def _(i):
-                    add(3 * (i // j), (i % j) * TILE, TILE)
+                    old_columns(j, 3 * i, j * TILE, ps_mid.at[2, i])
 
         n_slices = pieces * SUBS
 
@@ -328,7 +329,7 @@
                 @pl.when(jnp.logical_or(first, s == SUBS - 1))
                 def _():
                     wait_partner(zq, jq)
-                    expand(zq, jq, ps_mid.at[zq - 1, :, cols(jq)])
+                    expand(zq, jq, ps_mid.at[0, zq - 1, :, cols(jq)])
 
         send_sums(0)
 
@@ -362,12 +363,20 @@
             finish_edge(j)
             new_columns(j)
 
+        def old(j):
+            old_mid(j)
+            old_edge(j)
+
         def idle():
             pass
 
+        def second_piece():
+            edge_start(1)
+            old(1)
+
         edge_step(0, idle, mid_start, idle)
-        edge_step(1, lambda: mid_by_mid(2), lambda: edge_start(0), idle)
-        edge_step(2, lambda: old_columns(0), lambda: edge_start(1), lambda: old_columns(1))
+        edge_step(1, lambda: mid_by_mid(2), lambda: edge_start(0), lambda: old(0))
+        edge_step(2, idle, second_piece, idle)
 
         last = pieces - 1
 
@@ -380,45 +389,59 @@
         edge_start(last - 1)
         last_piece(zco)
         send_sums(pieces)
-        old_columns(last - 1)
-        edge_start(last)
-        old_columns(last)
-
-        @pl.loop(0, n_col)
-        def _(zq):
-            for j in range(pieces):
-                square(zq, j, ps.at[0, zq, :, cols(j)])
-
-        send_sums(pieces + 1)
-        sc[...] = scales(pieces + 1)
-
-        @pl.loop(0, n_col)
-        def _(zq):
-            a[:, quarter(zq)] = (acc[zq] * sc[zq]).astype(jnp.bfloat16)
-
-        @pl.loop(0, pieces)
+        old(last - 1)
+        finish_edge(last)
+        old_mid(last)
+        send_sums(second_mid)
+        new_columns(last)
+        old_edge(last)
+        send_sums(second_edge)
+
+        def finish_second(i, *quarters):
+            scale = scales(i)
+            for idx, zq in enumerate(quarters):
+                a[:, quarter(zq)] = (acc[zq] * scale[idx]).astype(jnp.bfloat16)
+
+        finish_second(second_mid, 1, 2)
+
+        @pl.loop(0, 2)
+        def _(i):
+            acc[zm, :, cols(i)] = two_quarters(a, zc + i * (zco - zc), blk, 0, 1, 2)
+
+        finish_second(second_edge, 0, 3)
+
+        def send_result(i, zq, j):
+            done = acc.at[zq, :, cols(j)]
+
+            @pl.when(i == 0)
+            def _():
+                remote(done, m_out.at[out_rows(side), cols(j)], fin_send.at[1], fin_recv.at[1, j], corner).start()
+
+            @pl.when(i == 1)
+            def _():
+                remote(done, fin.at[:, cols(j)], fin_send.at[0], fin_recv.at[2, j], other).start()
+
+        @pl.loop(0, 2)
+        def _(i):
+            zq = zc + i * (zco - zc)
+            square(acc[zm, :, cols(i)] + two_quarters(a, zq, blk, 0, 0, 3), zq, cols(0), ps.at[zq, :, cols(0)])
+            send_result(i, zq, 0)
+
+        @pl.loop(1, pieces)
         def _(j):
             @pl.loop(0, 2)
             def _(i):
-                zq = zco + i * (zc - zco)
-                expand(zq, j, ps.at[1, zq, :, cols(j)])
-                done = acc.at[zq, :, cols(j)]
-
-                @pl.when(i == 0)
-                def _():
-                    remote(done, fin.at[:, cols(j)], fin_send.at[0], fin_recv.at[2, j], other).start()
-
-                @pl.when(i == 1)
-                def _():
-                    remote(done, m_out.at[out_rows(side), cols(j)], fin_send.at[1], fin_recv.at[1, j], corner).start()
+                zq = zc + i * (zco - zc)
+                expand(zq, j, ps.at[zq, :, cols(j)])
+                send_result(i, zq, j)
 
         @pl.loop(0, 2 * pieces)
         def _(i):
             zq = zmo + (i // pieces) * (zm - zmo)
             j = i % pieces
-            expand(zq, j, ps.at[1, zq, :, cols(j)])
-
-        send_sums(pieces + 2)
+            expand(zq, j, ps.at[zq, :, cols(j)])
+
+        send_sums(third)
         remote(acc.at[zmo], m_out.at[out_rows(side), :], fin_send.at[2], fin_recv.at[0, 0], other).start()
         m_out[out_rows(side), :] = acc[zm]
 
@@ -428,7 +451,7 @@
             wait_for(ref, fin_recv.at[2, j])
             remote(ref, m_out.at[out_rows(1 - side), cols(j)], fin_send.at[3], fin_recv.at[2, j], corner).start()
 
-        sc[...] = scales(pieces + 2)
+        sc[...] = scales(third)
         remote(sc.at[zc], s_out, sc_sem.at[0], sc_sem.at[1], corner).start()
         s_out[...] = sc[zm]
 
@@ -437,7 +460,7 @@
         wait_sent(g.at[0, pl.ds(0, 3 * blk), :], send_sem.at[1])
         for zq in range(n_col):
             wait_sent(g.at[0, pl.ds(0, 2 * blk), :], send_sem.at[4 + zq])
-        for i in range(pieces + 3):
+        for i in range(len(exchanges)):
             wait_sent(peer_slots(i), ar_send.at[i])
         for i in range(4):
             wait_sent(acc.at[0], fin_send.at[i])
@@ -470,12 +493,12 @@
                 pltpu.VMEM((2, half, blk), jnp.bfloat16),
                 pltpu.VMEM((num_cols, half, blk), jnp.float32),
                 pltpu.VMEM((half, blk), jnp.float32),
-                pltpu.VMEM((2, 1, blk), jnp.float32),
-                pltpu.VMEM((cores, 2, 1, blk), jnp.float32),
+                pltpu.VMEM((3, 2, 1, blk), jnp.float32),
+                pltpu.VMEM((3, cores, 2, 1, blk), jnp.float32),
                 pltpu.VMEM((pieces, 2, 1, TILE), jnp.float32),
                 pltpu.VMEM((pieces, cores, 2, 1, TILE), jnp.float32),
-                pltpu.VMEM((2, num_cols, 1, blk), jnp.float32),
-                pltpu.VMEM((2, cores, num_cols, 1, blk), jnp.float32),
+                pltpu.VMEM((num_cols, 1, blk), jnp.float32),
+                pltpu.VMEM((cores, num_cols, 1, blk), jnp.float32),
                 pltpu.VMEM((num_cols, 1, blk), jnp.float32),
                 pltpu.SemaphoreType.DMA((4,)),
                 pltpu.SemaphoreType.DMA((2, pieces, SUBS)),
@@ -486,8 +509,8 @@
                 pltpu.SemaphoreType.DMA((3,)),
                 pltpu.SemaphoreType.DMA((4 + num_cols,)),
                 pltpu.SemaphoreType.DMA((4,)),
-                pltpu.SemaphoreType.DMA((pieces + 3,)),
-                pltpu.SemaphoreType.DMA((pieces + 3,)),
+                pltpu.SemaphoreType.DMA((pieces + 4,)),
+                pltpu.SemaphoreType.DMA((pieces + 4,)),
                 pltpu.SemaphoreType.DMA((3, pieces)),
                 pltpu.SemaphoreType.DMA((2,)),
             ],

time: 266 us -> 261 us (0.981)
  Pallas kernels: 263 us -> 258 us
    pallas_call x1, Pallas kernels: 263 us -> 258 us  [device_step(): pl.pallas_call(mcl_kernel, out_shape=(pltpu.VMEM((blk, blk), jnp.float32)...]
where the time goes in v6:
time: 261 us
  Pallas kernels  258 us (99%)
    pallas_call x1, Pallas kernels, device_step(): pl.pallas_call(mcl_kernel, out_shape=(pltpu.VMEM((blk, blk), jnp.float32)...  258 us

profile of v6, /device:TPU:0, one launch (start us, length us, event | category | flops | bytes accessed | tf_op | source)
XLA Modules:
  0.0 260.5 jit_solution(17137262770033003885)
XLA Ops:
  0.0 258.0 %shard_map.28 = (f32[1024,1024]{1,0:T(8,128)S(1)}, f32[1,1024]{1,0:T(1,128)S(1)}) custom-call(f32[1024,1024]{1,0:T(8,128)} %a_hbm.1, f32[1024,1024]{1,0:T(8,128)} %g_hbm.1), custom_call_target="tpu_custom_call" | custom-call | tf_op jit(solution)/shard_map/pallas_call | solution.py:484
  258.0 2.5 broadcast_multiply_fusion

commit v7 on v6

--- a/solution.py
+++ b/solution.py
@@ -8,7 +8,7 @@
 SUBS = 4
 TILE = 256
 AHEAD = 2
-LAG = 3
+LAG = 2
 MESH = pl.DeviceIdType.MESH
 
 
@@ -253,18 +253,22 @@
             @pl.loop(0, 2)
             def _(i):
                 zq = 3 * i
-                span = pl.ds(j * TILE, TILE)
-                total = (two_quarters(a1, zq, blk, j * TILE, 1, 2)
-                         + two_quarters(a1, zq, (j + 1) * TILE, j * TILE, 0, 3))
-                if j == pieces - 1:
-                    square(total, zq, span, ps_mid.at[2, i, :, span])
-                else:
-                    acc[zq, :, span] = total
+                acc[zq, :, pl.ds(j * TILE, TILE)] = (two_quarters(a1, zq, blk, j * TILE, 1, 2)
+                                                     + two_quarters(a1, zq, (j + 1) * TILE, j * TILE, 0, 3))
+
+        def last_new_columns(j):
+            @pl.loop(0, 2)
+            def _(i):
+                zq = 3 * i
+                fin[:, cols(i)] = (two_quarters(a1, zq, blk, j * TILE, 1, 2)
+                                   + two_quarters(a1, zq, j * TILE, j * TILE, 0, 3))
+
+        def piece_update(j, zq, n0, width):
+            return partial(a1, zq, j * TILE, TILE, n0, width) + partial(a1, zq, 3 * blk + j * TILE, TILE, n0, width)
 
         def old_columns(j, zq, width, slot):
             span = pl.ds(0, width)
-            total = (acc[zq, :, span] + partial(a1, zq, j * TILE, TILE, 0, width)
-                     + partial(a1, zq, 3 * blk + j * TILE, TILE, 0, width))
+            total = acc[zq, :, span] + piece_update(j, zq, 0, width)
             if j == pieces - 1:
                 square(total, zq, span, slot.at[:, span])
             else:
@@ -280,6 +284,11 @@
                 @pl.loop(0, 2)
                 def _(i):
                     old_columns(j, 3 * i, j * TILE, ps_mid.at[2, i])
+            if j == pieces - 1:
+                @pl.loop(0, 2)
+                def _(i):
+                    span = pl.ds(j * TILE, TILE)
+                    square(fin[:, cols(i)] + piece_update(j, 3 * i, j * TILE, TILE), 3 * i, span, ps_mid.at[2, i, :, span])
 
         n_slices = pieces * SUBS
 
@@ -333,27 +342,23 @@
 
         send_sums(0)
 
-        def edge_step(j, second, third, fourth):
+        def edge_step(j, tasks):
             @pl.loop(0, SUBS)
             def _(s):
                 pump((pieces + 1 + j) * SUBS + s)
 
-                @pl.when(jnp.logical_or(s == 0, s == SUBS - 1))
+                @pl.when(s % 2 == 0)
                 def _():
                     zq = jnp.where(s == 0, zc, zco)
                     wait_partner(zq, j)
                     expand(zq, j, ps_edge.at[j, zq // 3])
 
-                @pl.when(s == 1)
-                def _():
-                    second()
-
                 @pl.when(s == 2)
                 def _():
-                    third()
-
-            send_sums(1 + j)
-            fourth()
+                    send_sums(1 + j)
+
+                for at, task in tasks.items():
+                    pl.when(s == at)(task)
 
         def mid_start():
             finish_mid()
@@ -367,16 +372,13 @@
             old_mid(j)
             old_edge(j)
 
-        def idle():
-            pass
-
-        def second_piece():
-            edge_start(1)
-            old(1)
-
-        edge_step(0, idle, mid_start, idle)
-        edge_step(1, lambda: mid_by_mid(2), lambda: edge_start(0), lambda: old(0))
-        edge_step(2, idle, second_piece, idle)
+        def first_piece():
+            edge_start(0)
+            old(0)
+
+        edge_step(0, {3: mid_start})
+        edge_step(1, {1: lambda: mid_by_mid(2), 3: first_piece})
+        edge_step(2, {1: lambda: edge_start(1), 2: lambda: old(1)})
 
         last = pieces - 1
 
@@ -385,15 +387,16 @@
             expand(zq, last, ps_edge.at[last, zq // 3])
 
         last_piece(zc)
+        edge_start(last - 1)
         piece_across(2 * pieces - 1)
-        edge_start(last - 1)
+        old_mid(last - 1)
         last_piece(zco)
         send_sums(pieces)
-        old(last - 1)
+        old_edge(last - 1)
+        last_new_columns(last)
         finish_edge(last)
         old_mid(last)
         send_sums(second_mid)
-        new_columns(last)
         old_edge(last)
         send_sums(second_edge)
 

time: 261 us -> 259 us (level)
  no operation moved by 1% of the time
where the time goes in v7:
time: 259 us
  Pallas kernels  257 us (99%)
    pallas_call x1, Pallas kernels, device_step(): pl.pallas_call(mcl_kernel, out_shape=(pltpu.VMEM((blk, blk), jnp.float32)...  257 us

profile of v7, /device:TPU:0, one launch (start us, length us, event | category | flops | bytes accessed | tf_op | source)
XLA Modules:
  0.0 259.3 jit_solution(9113449389948853974)
XLA Ops:
  0.0 256.8 %shard_map.28 = (f32[1024,1024]{1,0:T(8,128)S(1)}, f32[1,1024]{1,0:T(1,128)S(1)}) custom-call(f32[1024,1024]{1,0:T(8,128)} %a_hbm.1, f32[1024,1024]{1,0:T(8,128)} %g_hbm.1), custom_call_target="tpu_custom_call" | custom-call | tf_op jit(solution)/shard_map/pallas_call | solution.py:487
  256.8 2.5 broadcast_multiply_fusion

commit v8 on v7

--- a/solution.py
+++ b/solution.py
@@ -7,7 +7,7 @@
 
 SUBS = 4
 TILE = 256
-AHEAD = 2
+AHEAD = 3
 LAG = 2
 MESH = pl.DeviceIdType.MESH
 
@@ -253,6 +253,8 @@
             @pl.loop(0, 2)
             def _(i):
                 zq = 3 * i
+                if j == pieces - 2:
+                    pl.when(i == 1)(lambda: piece_across(2 * pieces - 1))
                 acc[zq, :, pl.ds(j * TILE, TILE)] = (two_quarters(a1, zq, blk, j * TILE, 1, 2)
                                                      + two_quarters(a1, zq, (j + 1) * TILE, j * TILE, 0, 3))
 
@@ -378,7 +380,8 @@
 
         edge_step(0, {3: mid_start})
         edge_step(1, {1: lambda: mid_by_mid(2), 3: first_piece})
-        edge_step(2, {1: lambda: edge_start(1), 2: lambda: old(1)})
+        edge_step(2, {1: lambda: edge_start(1)})
+        old(1)
 
         last = pieces - 1
 
@@ -388,7 +391,6 @@
 
         last_piece(zc)
         edge_start(last - 1)
-        piece_across(2 * pieces - 1)
         old_mid(last - 1)
         last_piece(zco)
         send_sums(pieces)

time: 259 us -> 259 us (level)
  no operation moved by 1% of the time
where the time goes in v8:
time: 259 us; the launch traced here: 258 us
  Pallas kernels  256 us (99%)
    pallas_call x1, Pallas kernels, device_step(): pl.pallas_call(mcl_kernel, out_shape=(pltpu.VMEM((blk, blk), jnp.float32)...  256 us

profile of v8, /device:TPU:0, one launch (start us, length us, event | category | flops | bytes accessed | tf_op | source)
XLA Modules:
  0.0 258.1 jit_solution(6880951691397956440)
XLA Ops:
  0.0 255.6 %shard_map.28 = (f32[1024,1024]{1,0:T(8,128)S(1)}, f32[1,1024]{1,0:T(1,128)S(1)}) custom-call(f32[1024,1024]{1,0:T(8,128)} %a_hbm.1, f32[1024,1024]{1,0:T(8,128)} %g_hbm.1), custom_call_target="tpu_custom_call" | custom-call | tf_op jit(solution)/shard_map/pallas_call | solution.py:489
  255.6 2.5 broadcast_multiply_fusion

commit v9 on v8

--- a/solution.py
+++ b/solution.py
@@ -5,10 +5,10 @@
 from jax.experimental.pallas import tpu as pltpu
 from jax.sharding import PartitionSpec as P
 
-SUBS = 4
+SUBS = 8
 TILE = 256
-AHEAD = 3
-LAG = 2
+AHEAD = 6
+LAG = 4
 MESH = pl.DeviceIdType.MESH
 
 
@@ -21,6 +21,7 @@
     pieces = blk // TILE
     rows_s = blk // SUBS
     rows_a = half // SUBS
+    turn = SUBS // 4
 
     z = lax.axis_index("col")
     r = lax.axis_index("row")
@@ -335,9 +336,9 @@
                 pump(q * SUBS + s)
                 first = q == 0
                 zq = jnp.where(first, zm, zmo)
-                jq = jnp.where(first, s, q - 1)
-
-                @pl.when(jnp.logical_or(first, s == SUBS - 1))
+                jq = jnp.where(first, s // turn, q - 1)
+
+                @pl.when(jnp.logical_or(jnp.logical_and(first, s % turn == turn - 1), s == SUBS - 1))
                 def _():
                     wait_partner(zq, jq)
                     expand(zq, jq, ps_mid.at[0, zq - 1, :, cols(jq)])
@@ -349,18 +350,18 @@
             def _(s):
                 pump((pieces + 1 + j) * SUBS + s)
 
-                @pl.when(s % 2 == 0)
+                @pl.when(s % (2 * turn) == turn - 1)
                 def _():
-                    zq = jnp.where(s == 0, zc, zco)
+                    zq = jnp.where(s == turn - 1, zc, zco)
                     wait_partner(zq, j)
                     expand(zq, j, ps_edge.at[j, zq // 3])
 
-                @pl.when(s == 2)
+                @pl.when(s == 3 * turn - 1)
                 def _():
                     send_sums(1 + j)
 
                 for at, task in tasks.items():
-                    pl.when(s == at)(task)
+                    pl.when(s == (at + 1) * turn - 1)(task)
 
         def mid_start():
             finish_mid()

time: 259 us -> 259 us (level)
  no operation moved by 1% of the time
where the time goes in v9:
time: 259 us; the launch traced here: 258 us
  Pallas kernels  256 us (99%)
    pallas_call x1, Pallas kernels, device_step(): pl.pallas_call(mcl_kernel, out_shape=(pltpu.VMEM((blk, blk), jnp.float32)...  256 us

profile of v9, /device:TPU:0, one launch (start us, length us, event | category | flops | bytes accessed | tf_op | source)
XLA Modules:
  0.0 258.4 jit_solution(9497975590487290553)
XLA Ops:
  0.0 255.9 %shard_map.28 = (f32[1024,1024]{1,0:T(8,128)S(1)}, f32[1,1024]{1,0:T(1,128)S(1)}) custom-call(f32[1024,1024]{1,0:T(8,128)} %a_hbm.1, f32[1024,1024]{1,0:T(8,128)} %g_hbm.1), custom_call_target="tpu_custom_call" | custom-call | tf_op jit(solution)/shard_map/pallas_call | solution.py:490
  255.9 2.5 broadcast_multiply_fusion

commit v10 on v9

--- a/solution.py
+++ b/solution.py
@@ -5,10 +5,10 @@
 from jax.experimental.pallas import tpu as pltpu
 from jax.sharding import PartitionSpec as P
 
-SUBS = 8
+SUBS = 4
 TILE = 256
-AHEAD = 6
-LAG = 4
+AHEAD = 3
+LAG = 2
 MESH = pl.DeviceIdType.MESH
 
 
@@ -102,9 +102,10 @@
         return pltpu.make_async_copy(src.at[out_rows(h), :], acc.at[slot], load_sem.at[slot])
 
     loads = (load(a_hbm, 1 - side, 0), load(g_hbm, 0, 1), load(g_hbm, 1, 2), load(a_hbm, side, 3))
-    for copy in loads:
+    loads[0].start()
+    loads[0].wait()
+    for copy in loads[1:]:
         copy.start()
-    loads[0].wait()
     snd[0] = acc[0].astype(jnp.bfloat16)
     pl.semaphore_wait(barrier, jnp.where(middle, 2 * n_col, 2))
 
@@ -192,13 +193,16 @@
                 total = total + slots[peer]
             return n / total
 
-        def square(value, zq, span, slot):
+        def square(value, zq, span, slot, keep=None):
             value = value * value
-            acc[zq, :, span] = value
+            if keep is None:
+                acc[zq, :, span] = value
+            else:
+                fin[:, keep] = value
             slot[...] = jnp.sum(value, axis=0, keepdims=True)
 
-        def expand(zq, j, slot):
-            square(jnp.dot(a[...], g[zq, :, cols(j)], preferred_element_type=jnp.float32), zq, cols(j), slot)
+        def expand(zq, j, slot, keep=None):
+            square(jnp.dot(a[...], g[zq, :, cols(j)], preferred_element_type=jnp.float32), zq, cols(j), slot, keep)
 
         @pl.loop(0, pieces)
         def _(j):
@@ -233,8 +237,8 @@
         def finish_edge(j):
             scale = scales(1 + j)
             for idx, zq in ((0, 0), (1, 3)):
-                a1[:, pl.ds(zq * blk + j * TILE, TILE)] = (
-                    acc[zq, :, pl.ds(j * TILE, TILE)] * scale[idx]).astype(jnp.bfloat16)
+                kept = fin[:, cols(idx)] if j == pieces - 1 else acc[zq, :, pl.ds(j * TILE, TILE)]
+                a1[:, pl.ds(zq * blk + j * TILE, TILE)] = (kept * scale[idx]).astype(jnp.bfloat16)
 
         def partial(rows, zq, k0, k_len, n0, n_len):
             k = pl.ds(pl.multiple_of(k0, TILE), k_len)
@@ -263,7 +267,7 @@
             @pl.loop(0, 2)
             def _(i):
                 zq = 3 * i
-                fin[:, cols(i)] = (two_quarters(a1, zq, blk, j * TILE, 1, 2)
+                acc[zq, :, cols(j)] = (two_quarters(a1, zq, blk, j * TILE, 1, 2)
                                    + two_quarters(a1, zq, j * TILE, j * TILE, 0, 3))
 
         def piece_update(j, zq, n0, width):
@@ -286,29 +290,25 @@
             if j:
                 @pl.loop(0, 2)
                 def _(i):
-                    old_columns(j, 3 * i, j * TILE, ps_mid.at[2, i])
-            if j == pieces - 1:
-                @pl.loop(0, 2)
-                def _(i):
-                    span = pl.ds(j * TILE, TILE)
-                    square(fin[:, cols(i)] + piece_update(j, 3 * i, j * TILE, TILE), 3 * i, span, ps_mid.at[2, i, :, span])
+                    old_columns(j, 3 * i, blk if j == pieces - 1 else j * TILE, ps_mid.at[2, i])
 
         n_slices = pieces * SUBS
 
         def from_other(q):
             return zmo + (q // pieces) * (zco - zmo)
+
+        def relay_ahead(i):
+            ahead = i + AHEAD - n_slices
+
+            @pl.when(jnp.logical_and(ahead >= 0, ahead < n_slices))
+            def _():
+                ref = g_sub(zc, r, ahead // SUBS, ahead % SUBS)
+                copy_to(ref, send_sem.at[0], rm.at[1, ahead // SUBS, ahead % SUBS], other)
 
         def pump(i):
             q, s = i // SUBS, i % SUBS
             late, j = q // pieces, q % pieces
             z_m = from_other(q)
-            ahead = i + AHEAD - n_slices
-
-            @pl.when(jnp.logical_and(ahead >= 0, ahead < n_slices))
-            def _():
-                ref = g_sub(zc, r, ahead // SUBS, ahead % SUBS)
-                copy_to(ref, send_sem.at[0], rm.at[1, ahead // SUBS, ahead % SUBS], other)
-
             ref = g_sub(z_m, r, j, s)
             wait_for(ref, rm.at[late, j, s])
             copy_to(ref, send_sem.at[1], ry.at[1 + late, j], across)
@@ -333,6 +333,7 @@
         def _(q):
             @pl.loop(0, SUBS)
             def _(s):
+                relay_ahead(q * SUBS + s)
                 pump(q * SUBS + s)
                 first = q == 0
                 zq = jnp.where(first, zm, zmo)
@@ -348,7 +349,9 @@
         def edge_step(j, tasks):
             @pl.loop(0, SUBS)
             def _(s):
-                pump((pieces + 1 + j) * SUBS + s)
+                i = (pieces + 1 + j) * SUBS + s
+                pl.when(s != 3 * turn - 1)(lambda: relay_ahead(i))
+                pump(i)
 
                 @pl.when(s % (2 * turn) == turn - 1)
                 def _():
@@ -359,6 +362,7 @@
                 @pl.when(s == 3 * turn - 1)
                 def _():
                     send_sums(1 + j)
+                    relay_ahead(i)
 
                 for at, task in tasks.items():
                     pl.when(s == (at + 1) * turn - 1)(task)
@@ -388,7 +392,7 @@
 
         def last_piece(zq):
             wait_partner(zq, last)
-            expand(zq, last, ps_edge.at[last, zq // 3])
+            expand(zq, last, ps_edge.at[last, zq // 3], cols(zq // 3))
 
         last_piece(zc)
         edge_start(last - 1)

time: 259 us -> 258 us (level)
  no operation moved by 1% of the time
where the time goes in v10:
time: 258 us
  Pallas kernels  255 us (99%)
    pallas_call x1, Pallas kernels, device_step(): pl.pallas_call(mcl_kernel, out_shape=(pltpu.VMEM((blk, blk), jnp.float32)...  255 us

profile of v10, /device:TPU:0, one launch (start us, length us, event | category | flops | bytes accessed | tf_op | source)
XLA Modules:
  0.0 257.9 jit_solution(12606081603374759179)
XLA Ops:
  0.0 255.4 %shard_map.28 = (f32[1024,1024]{1,0:T(8,128)S(1)}, f32[1,1024]{1,0:T(1,128)S(1)}) custom-call(f32[1024,1024]{1,0:T(8,128)} %a_hbm.1, f32[1024,1024]{1,0:T(8,128)} %g_hbm.1), custom_call_target="tpu_custom_call" | custom-call | tf_op jit(solution)/shard_map/pallas_call | solution.py:494
  255.4 2.5 broadcast_multiply_fusion

commit v11 on v10

--- a/solution.py
+++ b/solution.py
@@ -102,10 +102,9 @@
         return pltpu.make_async_copy(src.at[out_rows(h), :], acc.at[slot], load_sem.at[slot])
 
     loads = (load(a_hbm, 1 - side, 0), load(g_hbm, 0, 1), load(g_hbm, 1, 2), load(a_hbm, side, 3))
-    loads[0].start()
+    for copy in loads:
+        copy.start()
     loads[0].wait()
-    for copy in loads[1:]:
-        copy.start()
     snd[0] = acc[0].astype(jnp.bfloat16)
     pl.semaphore_wait(barrier, jnp.where(middle, 2 * n_col, 2))
 
@@ -166,7 +165,7 @@
             for dz in range(2):
                 for dr in range(n_col):
                     if dz or dr:
-                        yield (zmo if dz else zm), (r + dr) % n_col
+                        yield dz == 0, (zmo if dz else zm), (r + dr) % n_col
 
         exchanges = [(ps_mid.at[0], ar_mid.at[0])]
         exchanges += [(ps_edge.at[j], ar_edge.at[j]) for j in range(pieces)]
@@ -178,9 +177,10 @@
 
         def send_sums(i):
             src, slots = sums_of(i)
-            for pz, pr in peers():
-                remote(src, slots.at[me], ar_send.at[i], ar_recv.at[i], dev(pz, pr)).start()
-            slots[me] = src[...]
+            for same, pz, pr in peers():
+                part = src.at[side if same else 1 - side] if i == third else src
+                remote(part, slots.at[me], ar_send.at[i], ar_recv.at[i], dev(pz, pr)).start()
+            slots[me] = src[side] if i == third else src[...]
 
         def peer_slots(i):
             return sums_of(i)[1].at[pl.ds(0, 2 * n_col - 1)]
@@ -258,8 +258,6 @@
             @pl.loop(0, 2)
             def _(i):
                 zq = 3 * i
-                if j == pieces - 2:
-                    pl.when(i == 1)(lambda: piece_across(2 * pieces - 1))
                 acc[zq, :, pl.ds(j * TILE, TILE)] = (two_quarters(a1, zq, blk, j * TILE, 1, 2)
                                                      + two_quarters(a1, zq, (j + 1) * TILE, j * TILE, 0, 3))
 
@@ -396,6 +394,7 @@
 
         last_piece(zc)
         edge_start(last - 1)
+        piece_across(2 * pieces - 1)
         old_mid(last - 1)
         last_piece(zco)
         send_sums(pieces)
@@ -420,6 +419,9 @@
 
         finish_second(second_edge, 0, 3)
 
+        def last_sums(zq, j):
+            return ps.at[zq // 2, jnp.where(zq % 3 == 0, 1, 0), :, cols(j)]
+
         def send_result(i, zq, j):
             done = acc.at[zq, :, cols(j)]
 
@@ -434,7 +436,7 @@
         @pl.loop(0, 2)
         def _(i):
             zq = zc + i * (zco - zc)
-            square(acc[zm, :, cols(i)] + two_quarters(a, zq, blk, 0, 0, 3), zq, cols(0), ps.at[zq, :, cols(0)])
+            square(acc[zm, :, cols(i)] + two_quarters(a, zq, blk, 0, 0, 3), zq, cols(0), last_sums(zq, 0))
             send_result(i, zq, 0)
 
         @pl.loop(1, pieces)
@@ -442,14 +444,14 @@
             @pl.loop(0, 2)
             def _(i):
                 zq = zc + i * (zco - zc)
-                expand(zq, j, ps.at[zq, :, cols(j)])
+                expand(zq, j, last_sums(zq, j))
                 send_result(i, zq, j)
 
         @pl.loop(0, 2 * pieces)
         def _(i):
             zq = zmo + (i // pieces) * (zm - zmo)
             j = i % pieces
-            expand(zq, j, ps.at[zq, :, cols(j)])
+            expand(zq, j, last_sums(zq, j))
 
         send_sums(third)
         remote(acc.at[zmo], m_out.at[out_rows(side), :], fin_send.at[2], fin_recv.at[0, 0], other).start()
@@ -462,8 +464,8 @@
             remote(ref, m_out.at[out_rows(1 - side), cols(j)], fin_send.at[3], fin_recv.at[2, j], corner).start()
 
         sc[...] = scales(third)
-        remote(sc.at[zc], s_out, sc_sem.at[0], sc_sem.at[1], corner).start()
-        s_out[...] = sc[zm]
+        remote(sc.at[1], s_out, sc_sem.at[0], sc_sem.at[1], corner).start()
+        s_out[...] = sc[0]
 
         wait_sent(snd, send_sem.at[3])
         wait_sent(g.at[0, pl.ds(0, 2 * blk), :], send_sem.at[0])
@@ -507,9 +509,9 @@
                 pltpu.VMEM((3, cores, 2, 1, blk), jnp.float32),
                 pltpu.VMEM((pieces, 2, 1, TILE), jnp.float32),
                 pltpu.VMEM((pieces, cores, 2, 1, TILE), jnp.float32),
-                pltpu.VMEM((num_cols, 1, blk), jnp.float32),
-                pltpu.VMEM((cores, num_cols, 1, blk), jnp.float32),
-                pltpu.VMEM((num_cols, 1, blk), jnp.float32),
+                pltpu.VMEM((2, 2, 1, blk), jnp.float32),
+                pltpu.VMEM((cores, 2, 1, blk), jnp.float32),
+                pltpu.VMEM((2, 1, blk), jnp.float32),
                 pltpu.SemaphoreType.DMA((4,)),
                 pltpu.SemaphoreType.DMA((2, pieces, SUBS)),
                 pltpu.SemaphoreType.DMA((2, pieces)),

time: 258 us -> 258 us (level)
  no operation moved by 1% of the time
where the time goes in v11:
time: 258 us
  Pallas kernels  255 us (99%)
    pallas_call x1, Pallas kernels, device_step(): pl.pallas_call(mcl_kernel, out_shape=(pltpu.VMEM((blk, blk), jnp.float32)...  255 us

profile of v11, /device:TPU:0, one launch (start us, length us, event | category | flops | bytes accessed | tf_op | source)
XLA Modules:
  0.0 257.5 jit_solution(16674743608526530843)
XLA Ops:
  0.0 255.0 %shard_map.28 = (f32[1024,1024]{1,0:T(8,128)S(1)}, f32[1,1024]{1,0:T(1,128)S(1)}) custom-call(f32[1024,1024]{1,0:T(8,128)} %a_hbm.1, f32[1024,1024]{1,0:T(8,128)} %g_hbm.1), custom_call_target="tpu_custom_call" | custom-call | tf_op jit(solution)/shard_map/pallas_call | solution.py:496
  255.0 2.5 broadcast_multiply_fusion

commit v12 on v11

--- a/solution.py
+++ b/solution.py
@@ -12,7 +12,7 @@
 MESH = pl.DeviceIdType.MESH
 
 
-def mcl_kernel(a_hbm, g_hbm, m_out, s_out, g, a, a1, snd, acc, fin, ps_mid, ar_mid, ps_edge, ar_edge, ps, ar, sc,
+def mcl_kernel(a_hbm, g_hbm, out, g, a, a1, snd, acc, fin, ps_mid, ar_mid, ps_edge, ar_edge, ps, ar, sc,
                load_sem, rm, re, ry, rp, ra_relay, ra, send_sem, fin_send, ar_send, ar_recv, fin_recv, sc_sem):
     n_col = g.shape[0]
     blk = g.shape[2]
@@ -122,6 +122,10 @@
         loads[1 + h].wait()
         g[z, pl.ds(pl.multiple_of(r * blk + h * half, half), half), :] = acc[1 + h].astype(jnp.bfloat16)
 
+    def receive(kind, h, j, scale):
+        wait_for(out.at[out_rows(h), cols(j)], fin_recv.at[kind, j])
+        out[out_rows(h), cols(j)] = out[out_rows(h), cols(j)] * scale
+
     @pl.when(jnp.logical_not(middle))
     def _():
         inner = dev(zm, r)
@@ -147,12 +151,11 @@
         wait_sent(g_block(z, r), send_sem.at[1])
         wait_sent(g.at[0, pl.ds(0, 2 * blk), :], send_sem.at[2])
 
+        wait_for(sc.at[1], sc_sem.at[1])
         for kind, h in ((1, side), (2, 1 - side)):
             @pl.loop(0, pieces)
             def _(j):
-                wait_for(m_out.at[out_rows(h), cols(j)], fin_recv.at[kind, j])
-
-        wait_for(s_out, sc_sem.at[1])
+                receive(kind, h, j, sc[1, :, cols(j)])
 
     @pl.when(middle)
     def _():
@@ -383,8 +386,8 @@
 
         edge_step(0, {3: mid_start})
         edge_step(1, {1: lambda: mid_by_mid(2), 3: first_piece})
-        edge_step(2, {1: lambda: edge_start(1)})
-        old(1)
+        edge_step(2, {1: lambda: edge_start(1), 2: lambda: old_edge(1)})
+        old_mid(1)
 
         last = pieces - 1
 
@@ -427,7 +430,7 @@
 
             @pl.when(i == 0)
             def _():
-                remote(done, m_out.at[out_rows(side), cols(j)], fin_send.at[1], fin_recv.at[1, j], corner).start()
+                remote(done, out.at[out_rows(side), cols(j)], fin_send.at[1], fin_recv.at[1, j], corner).start()
 
             @pl.when(i == 1)
             def _():
@@ -454,18 +457,21 @@
             expand(zq, j, last_sums(zq, j))
 
         send_sums(third)
-        remote(acc.at[zmo], m_out.at[out_rows(side), :], fin_send.at[2], fin_recv.at[0, 0], other).start()
-        m_out[out_rows(side), :] = acc[zm]
+
+        @pl.loop(0, pieces)
+        def _(j):
+            remote(acc.at[zmo, :, cols(j)], out.at[out_rows(side), cols(j)], fin_send.at[2], fin_recv.at[0, j],
+                   other).start()
 
         @pl.loop(0, pieces)
         def _(j):
             ref = fin.at[:, cols(j)]
             wait_for(ref, fin_recv.at[2, j])
-            remote(ref, m_out.at[out_rows(1 - side), cols(j)], fin_send.at[3], fin_recv.at[2, j], corner).start()
+            remote(ref, out.at[out_rows(1 - side), cols(j)], fin_send.at[3], fin_recv.at[2, j], corner).start()
 
         sc[...] = scales(third)
-        remote(sc.at[1], s_out, sc_sem.at[0], sc_sem.at[1], corner).start()
-        s_out[...] = sc[0]
+        remote(sc.at[1], sc.at[1], sc_sem.at[0], sc_sem.at[1], corner).start()
+        out[out_rows(side), :] = acc[zm] * sc[0]
 
         wait_sent(snd, send_sem.at[3])
         wait_sent(g.at[0, pl.ds(0, 2 * blk), :], send_sem.at[0])
@@ -477,7 +483,10 @@
         for i in range(4):
             wait_sent(acc.at[0], fin_send.at[i])
         wait_sent(sc.at[0], sc_sem.at[0])
-        wait_for(m_out.at[out_rows(1 - side), :], fin_recv.at[0, 0])
+
+        @pl.loop(0, pieces)
+        def _(j):
+            receive(0, 1 - side, j, sc[0, :, cols(j)])
 
 
 def solution(mesh):
@@ -492,12 +501,11 @@
         pieces = blk // TILE
         cores = 2 * num_rows
         any_spec = pl.BlockSpec(memory_space=pl.ANY)
-        vmem_spec = pl.BlockSpec(memory_space=pltpu.VMEM)
-        squares, scale = pl.pallas_call(
+        return pl.pallas_call(
             mcl_kernel,
-            out_shape=(pltpu.VMEM((blk, blk), jnp.float32), pltpu.VMEM((1, blk), jnp.float32)),
+            out_shape=pltpu.VMEM((blk, blk), jnp.float32),
             in_specs=[any_spec, any_spec],
-            out_specs=(vmem_spec, vmem_spec),
+            out_specs=pl.BlockSpec(memory_space=pltpu.VMEM),
             scratch_shapes=[
                 pltpu.VMEM((num_cols, n, blk), jnp.bfloat16),
                 pltpu.VMEM((half, n), jnp.bfloat16),
@@ -529,6 +537,5 @@
             compiler_params=pltpu.CompilerParams(
                 collective_id=0, has_side_effects=True, vmem_limit_bytes=60_000_000),
         )(init_blk, graph_blk)
-        return squares * scale
 
     return jax.shard_map(device_step, mesh=mesh, in_specs=(block_spec, block_spec), out_specs=block_spec, check_vma=False)

time: 258 us -> 258 us (level)
  no operation moved by 1% of the time
where the time goes in v12:
time: 258 us
  Pallas kernels  255 us (99%)
    pallas_call x1, Pallas kernels, device_step(): pl.pallas_call(mcl_kernel, out_shape=pltpu.VMEM((blk, blk), jnp.float32),...  255 us

profile of v12, /device:TPU:0, one launch (start us, length us, event | category | flops | bytes accessed | tf_op | source)
XLA Modules:
  0.0 257.5 jit_solution(3072621741154412290)
XLA Ops:
  0.0 255.5 %shard_map.28 = f32[1024,1024]{1,0:T(8,128)S(1)} custom-call(f32[1024,1024]{1,0:T(8,128)} %a_hbm.1, f32[1024,1024]{1,0:T(8,128)} %g_hbm.1), custom_call_target="tpu_custom_call" | custom-call | tf_op jit(solution)/shard_map/pallas_call | solution.py:504
  255.5 2.0 copy.4

commit v13 on v11

--- a/solution.py
+++ b/solution.py
@@ -383,8 +383,8 @@
 
         edge_step(0, {3: mid_start})
         edge_step(1, {1: lambda: mid_by_mid(2), 3: first_piece})
-        edge_step(2, {1: lambda: edge_start(1)})
-        old(1)
+        edge_step(2, {1: lambda: edge_start(1), 2: lambda: old_edge(1)})
+        old_mid(1)
 
         last = pieces - 1
 

time: 258 us -> 258 us (level)
  no operation moved by 1% of the time
where the time goes in v13:
time: 258 us
  Pallas kernels  255 us (99%)
    pallas_call x1, Pallas kernels, device_step(): pl.pallas_call(mcl_kernel, out_shape=(pltpu.VMEM((blk, blk), jnp.float32)...  255 us

profile of v13, /device:TPU:0, one launch (start us, length us, event | category | flops | bytes accessed | tf_op | source)
XLA Modules:
  0.0 257.5 jit_solution(10238006820567050878)
XLA Ops:
  0.0 255.0 %shard_map.28 = (f32[1024,1024]{1,0:T(8,128)S(1)}, f32[1,1024]{1,0:T(1,128)S(1)}) custom-call(f32[1024,1024]{1,0:T(8,128)} %a_hbm.1, f32[1024,1024]{1,0:T(8,128)} %g_hbm.1), custom_call_target="tpu_custom_call" | custom-call | tf_op jit(solution)/shard_map/pallas_call | solution.py:496
  255.0 2.5 broadcast_multiply_fusion

commit v14 on v13

--- a/solution.py
+++ b/solution.py
@@ -249,8 +249,8 @@
             first, second = (partial(rows, zq, k * blk, k_len, n0, TILE) for k in k_z)
             return first + second
 
-        def mid_by_mid(zq):
-            @pl.loop(0, pieces)
+        def mid_by_mid(zq, j0, j1):
+            @pl.loop(j0, j1)
             def _(j):
                 acc[zq, :, cols(j)] = two_quarters(a1, zq, blk, j * TILE, 1, 2)
 
@@ -367,7 +367,7 @@
 
         def mid_start():
             finish_mid()
-            mid_by_mid(1)
+            mid_by_mid(1, 0, pieces // 2)
 
         def edge_start(j):
             finish_edge(j)
@@ -377,13 +377,10 @@
             old_mid(j)
             old_edge(j)
 
-        def first_piece():
-            edge_start(0)
-            old(0)
-
         edge_step(0, {3: mid_start})
-        edge_step(1, {1: lambda: mid_by_mid(2), 3: first_piece})
-        edge_step(2, {1: lambda: edge_start(1), 2: lambda: old_edge(1)})
+        edge_step(1, {0: lambda: mid_by_mid(1, pieces // 2, pieces), 1: lambda: mid_by_mid(2, 0, pieces),
+                      3: lambda: edge_start(0)})
+        edge_step(2, {0: lambda: old(0), 1: lambda: edge_start(1), 2: lambda: old_edge(1)})
         old_mid(1)
 
         last = pieces - 1

time: 258 us -> 258 us (level)
  no operation moved by 1% of the time
where the time goes in v14:
time: 258 us; the launch traced here: 257 us
  Pallas kernels  255 us (99%)
    pallas_call x1, Pallas kernels, device_step(): pl.pallas_call(mcl_kernel, out_shape=(pltpu.VMEM((blk, blk), jnp.float32)...  255 us

profile of v14, /device:TPU:0, one launch (start us, length us, event | category | flops | bytes accessed | tf_op | source)
XLA Modules:
  0.0 257.4 jit_solution(8790091669593555016)
XLA Ops:
  0.0 254.9 %shard_map.28 = (f32[1024,1024]{1,0:T(8,128)S(1)}, f32[1,1024]{1,0:T(1,128)S(1)}) custom-call(f32[1024,1024]{1,0:T(8,128)} %a_hbm.1, f32[1024,1024]{1,0:T(8,128)} %g_hbm.1), custom_call_target="tpu_custom_call" | custom-call | tf_op jit(solution)/shard_map/pallas_call | solution.py:493
  254.9 2.5 broadcast_multiply_fusion
